TPU v7x, 32 devices: a 4x4x1 block of a 4x4x8 slice. The times are simulated.
32 devices in a mesh: rep: 2 (over z, core), dp: 16 (over x, y).
Axes of the slice: x: 4, y: 4, z: 1, core: 2. Of those that a mesh axis runs over, the one named last changes fastest.
The devices are a block of a 4x4x8 slice.
Arguments:
- x: bfloat16 [32, 2048, 1024], P(('rep', 'dp')), parts along dimension 0
- dy: bfloat16 [32, 2048, 1024], P(('rep', 'dp')), parts along dimension 0
- w_gate: bfloat16 [2, 1024, 2816], replicated
- w_up: bfloat16 [2, 1024, 2816], replicated
- w_down: bfloat16 [2, 2816, 1024], replicated
- m_w_gate: float32 [2, 1024, 2816], P(None, 'dp')
- m_w_up: float32 [2, 1024, 2816], P(None, 'dp')
- m_w_down: float32 [2, 2816, 1024], P(None, 'dp')
- v_w_gate: float32 [2, 1024, 2816], P(None, 'dp')
- v_w_up: float32 [2, 1024, 2816], P(None, 'dp')
- v_w_down: float32 [2, 2816, 1024], P(None, 'dp')
Outputs:
- output 1: bfloat16 [4, 1024, 2816], P('rep'), parts along dimension 0
- output 2: bfloat16 [4, 1024, 2816], P('rep'), parts along dimension 0
- output 3: bfloat16 [4, 2816, 1024], P('rep'), parts along dimension 0
- output 4: float32 [4, 1024, 2816], P('rep', 'dp'), parts along dimension 0
- output 5: float32 [4, 1024, 2816], P('rep', 'dp'), parts along dimension 0
- output 6: float32 [4, 2816, 1024], P('rep', 'dp'), parts along dimension 0
- output 7: float32 [4, 1024, 2816], P('rep', 'dp'), parts along dimension 0
- output 8: float32 [4, 1024, 2816], P('rep', 'dp'), parts along dimension 0
- output 9: float32 [4, 2816, 1024], P('rep', 'dp'), parts along dimension 0
There are 2 independent parts. A program takes and returns all parts, laid end to end along the dimension named above; an argument that names none is the same for every part.
All inputs are finite; a program needn't handle non-finite values.
Results may differ from a plain program's by a relative error of at most 0.02.
Values are sent between devices in bfloat16 or wider.
A program may use at most 768 MiB of HBM per device.

v0:
```python
import jax
import jax.numpy as jnp
from jax import lax

NAMES = ("w_gate", "w_up", "w_down")


def matmul(a, w):
    return jnp.dot(a, w, preferred_element_type=jnp.float32).astype(jnp.bfloat16)


def normed(h):
    wide = h.astype(jnp.float32)
    scale = lax.rsqrt(jnp.mean(wide**2, -1, keepdims=True) + 1e-6)
    return (wide * scale).astype(jnp.bfloat16)


def layer(h, w):
    a = normed(h)
    gate = jnp.dot(a, w["w_gate"], preferred_element_type=jnp.float32)
    up = jnp.dot(a, w["w_up"], preferred_element_type=jnp.float32)
    return h + matmul((jax.nn.silu(gate) * up).astype(jnp.bfloat16), w["w_down"])


def adamw(w, m, v, g):
    m = 0.9 * m + 0.1 * g
    v = 0.95 * v + 0.05 * g * g
    step = m * lax.rsqrt(v + 1e-8) + 0.1 * w
    return (w - 0.02 * step).astype(jnp.bfloat16), m, v


def stack(weights, h):
    for number in range(weights["w_gate"].shape[0]):
        h = layer(h, {name: w[number] for name, w in weights.items()})
    return h


def solution(mesh):
    groups = mesh.shape["rep"]

    def step(x, dy, *arrays):
        weights, m, v = (arrays[i : i + 3] for i in (0, 3, 6))
        x, dy = (t.reshape(groups, -1, *t.shape[1:]) for t in (x, dy))

        def of_a_group(x, dy):
            _, back = jax.vjp(lambda w: stack(w, x), dict(zip(NAMES, weights, strict=True)))
            by_weights = back(dy)[0]
            gradients = [by_weights[name].astype(jnp.float32) for name in NAMES]
            new = [adamw(w.astype(jnp.float32), m, v, g) for w, m, v, g in zip(weights, m, v, gradients, strict=True)]
            return tuple(one[which] for which in range(3) for one in new)

        return tuple(t.reshape(-1, *t.shape[2:]) for t in jax.vmap(of_a_group)(x, dy))

    return step
```

profile of v0, /device:TPU:96, one launch (start us, length us, event | category | flops | bytes accessed | tf_op | source)
XLA Modules:
  0.0 996.5 jit_solution(14327904276330661205)
XLA Ops:
  7.3 3.1 fusion.35
  10.3 6.5 copy
  16.8 20.0 %fusion.67 = f32[2048,2816]{1,0:T(8,128)} fusion(bf16[2,1024,2816]{2,1,0:T(8,128)(2,1)} %param, bf16[1,2048,1024]{2,1,0:T(8,128)(2,1)} %param.2, f32[2048]{0:T(1024)S(1)} %add_rsqrt_fusion), kind=kOutput, calls=%fused_computation.79 | convolution fusion | flops 11817451520 | bytes 33038336 | tf_op jit(solution)/vmap(jvp())/dot_general | solution.py:20
  36.8 18.3 %fusion.65 = f32[2048,2816]{1,0:T(8,128)} fusion(bf16[2,1024,2816]{2,1,0:T(8,128)(2,1)} %param.3, bf16[1,2048,1024]{2,1,0:T(8,128)(2,1)S(1)} %copy-done.1, f32[2048]{0:T(1024)S(1)} %add_rsqrt_fusion), kind=kOutput, calls=%fused_computation.77 | convolution fusion | flops 11817451520 | bytes 33038336 | tf_op jit(solution)/vmap(jvp())/dot_general | solution.py:21
  55.1 19.6 %fusion.26 = bf16[2048,2816]{1,0:T(8,128)(2,1)} fusion(f32[2048,2816]{1,0:T(8,128)} %fusion.65, f32[2048,2816]{1,0:T(8,128)} %fusion.67), kind=kLoop, calls=%fused_computation.39 | loop fusion | flops 34603008 | bytes 57671680
  74.7 19.9 %fusion.39 = (f32[2048]{0:T(1024)S(1)}, bf16[1,1,2048,1024]{2,3,1,0:T(8,128)(2,1)}) fusion(bf16[2048,2816]{1,0:T(8,128)(2,1)} %fusion.26, bf16[2,2816,1024]{2,1,0:T(8,128)(2,1)} %param.4, bf16[1,2048,1024]{1,2,0:T(8,128)(2,1)} %copy), kind=kOutput, calls=%fused_computation.56 | convolution fusion | flops 11821643776 | bytes 25698304 | tf_op jit(solution)/vmap(jvp())/dot_general | solution.py:9
  94.6 0.6 copy-done.13
  95.2 20.2 %fusion.54 = f32[2048,2816]{1,0:T(8,128)} fusion(bf16[2,1024,2816]{2,1,0:T(8,128)(2,1)} %param, bf16[1,1,2048,1024]{2,3,1,0:T(8,128)(2,1)} %get-tuple-element.10, f32[2048]{0:T(1024)S(1)} %bitcast.337), kind=kOutput, calls=%fused_computation.66 | convolution fusion | flops 11817451520 | bytes 33038336 | tf_op jit(solution)/vmap(jvp())/dot_general | solution.py:20
  115.4 18.2 %fusion.58 = f32[2048,2816]{1,0:T(8,128)} fusion(bf16[2,1024,2816]{2,1,0:T(8,128)(2,1)} %param.3, bf16[1,1,2048,1024]{2,3,1,0:T(8,128)(2,1)S(1)} %copy-done.4, f32[2048]{0:T(1024)S(1)} %bitcast.338), kind=kOutput, calls=%fused_computation.70 | convolution fusion | flops 11817451520 | bytes 33038336 | tf_op jit(solution)/vmap(jvp())/dot_general | solution.py:21
  133.6 24.2 %fusion.48 = f32[1,2816,1024]{2,1,0:T(8,128)} fusion(f32[2048,2816]{1,0:T(8,128)} %fusion.58, f32[2048,2816]{1,0:T(8,128)} %fusion.54, bf16[1,2048,1024]{2,1,0:T(8,128)(2,1)S(1)} %copy-done.7), kind=kOutput, calls=%fused_computation.62 | convolution fusion | flops 11845763072 | bytes 61865984 | tf_op jit(solution)/vmap(transpose(jvp()))/dot_general | solution.py:9
  157.9 0.1 reduce-scatter.29.cloned.1.call-start
  157.9 6.8 copy.1
  164.7 18.1 %convolution_convert_fusion.1 = bf16[2048,2816]{1,0:T(8,128)(2,1)} fusion(bf16[2,2816,1024]{2,1,0:T(8,128)(2,1)} %param.4, bf16[1,2048,1024]{2,1,0:T(8,128)(2,1)} %param.5), kind=kOutput, calls=%fused_computation.48 | convolution fusion | flops 11816927232 | bytes 21495808 | tf_op jit(solution)/vmap(transpose(jvp()))/dot_general | solution.py:9
  182.9 23.4 %fusion.6 = bf16[2048,2816]{1,0:T(8,128)(2,1)} fusion(f32[2048,2816]{1,0:T(8,128)} %fusion.54, f32[2048,2816]{1,0:T(8,128)} %fusion.58, bf16[2048,2816]{1,0:T(8,128)(2,1)} %convolution_convert_fusion.1), kind=kLoop, calls=%fused_computation.11 | loop fusion | flops 69206016 | bytes 69206016
  206.3 1.5 copy-done.3
  207.8 20.4 %fusion.24 = bf16[2048,1024]{0,1:T(8,128)(2,1)} fusion(bf16[2048,2816]{1,0:T(8,128)(2,1)S(1)} %copy-done.3, f32[2048,2816]{1,0:T(8,128)} %fusion.54, bf16[2,1024,2816]{2,1,0:T(8,128)(2,1)} %param.3), kind=kOutput, calls=%fused_computation.34 | convolution fusion | flops 11845763072 | bytes 44564480 | tf_op jit(solution)/vmap(transpose(jvp()))/dot_general | solution.py:21
  228.2 20.7 %fusion.41 = (f32[2048]{0:T(1024)S(1)}, bf16[2048,1024]{0,1:T(8,128)(2,1)}) fusion(bf16[1,1,2048,1024]{2,3,1,0:T(8,128)(2,1)} %get-tuple-element.10, bf16[2048,1024]{0,1:T(8,128)(2,1)} %fusion.24, bf16[2048,2816]{1,0:T(8,128)(2,1)} %fusion.6, bf16[2,1024,2816]{2,1,0:T(8,128)(2,1)} %param), kind=kOutput, calls=%fused_computation.58 | convolution fusion | flops 11821643776 | bytes 29892608 | tf_op jit(solution)/vmap(transpose(jvp()))/dot_general | solution.py:20
  249.0 4.7 fusion.81
  253.8 1.9 copy-done.6
  255.7 17.7 %convolution_bitcast_fusion = f32[1,2816,1024]{2,1,0:T(8,128)} fusion(bf16[2048,2816]{1,0:T(8,128)(2,1)} %fusion.26, bf16[2048,1024]{0,1:T(8,128)(2,1)S(1)} %fusion.81), kind=kOutput, calls=%fused_computation.63 | convolution fusion | flops 11811160064 | bytes 27262976 | tf_op jit(solution)/vmap(transpose(jvp()))/dot_general | solution.py:9
  273.5 18.9 %convolution_bitcast_fusion.1 = f32[1,1024,2816]{2,1,0:T(8,128)} fusion(bf16[2048,2816]{1,0:T(8,128)(2,1)} %fusion.6, bf16[1,1,2048,1024]{2,3,1,0:T(8,128)(2,1)} %get-tuple-element.10, f32[2048]{0:T(1024)S(1)} %bitcast.340), kind=kOutput, calls=%fused_computation.64 | convolution fusion | flops 11817451520 | bytes 27271168 | tf_op jit(solution)/vmap(transpose(jvp()))/dot_general | solution.py:20
  292.6 18.4 %convolution_convert_fusion = bf16[2048,2816]{1,0:T(8,128)(2,1)} fusion(bf16[2048,1024]{0,1:T(8,128)(2,1)} %copy-done.6, bf16[2,2816,1024]{2,1,0:T(8,128)(2,1)} %param.4), kind=kOutput, calls=%fused_computation.47 | convolution fusion | flops 11816927232 | bytes 21495808 | tf_op jit(solution)/vmap(transpose(jvp()))/dot_general | solution.py:9
  311.0 26.1 %fusion.51 = f32[1,1024,2816]{2,1,0:T(8,128)} fusion(f32[2048,2816]{1,0:T(8,128)} %fusion.67, f32[2048,2816]{1,0:T(8,128)} %fusion.65, bf16[2048,2816]{1,0:T(8,128)(2,1)} %convolution_convert_fusion, bf16[1,2048,1024]{1,2,0:T(8,128)(2,1)S(1)} %copy-done.8, f32[2048]{0:T(1024)S(1)} %copy-done.18), kind=kOutput, calls=%fused_computation.65 | convolution fusion | flops 11880890368 | bytes 73408512 | tf_op jit(solution)/vmap(transpose(jvp()))/dot_general | solution.py:20
  337.2 23.5 %fusion.42 = f32[1,1024,2816]{2,1,0:T(8,128)} fusion(bf16[2048,2816]{1,0:T(8,128)(2,1)} %convolution_convert_fusion.1, f32[2048,2816]{1,0:T(8,128)} %fusion.54, bf16[1,1,2048,1024]{2,3,1,0:T(8,128)(2,1)} %get-tuple-element.10, f32[2048]{0:T(1024)S(1)} %bitcast.341), kind=kOutput, calls=%fused_computation.60 | convolution fusion | flops 11852054528 | bytes 50339840 | tf_op jit(solution)/vmap(transpose(jvp()))/dot_general | solution.py:21
  360.9 23.7 %fusion.45 = f32[1,1024,2816]{2,1,0:T(8,128)} fusion(bf16[2048,2816]{1,0:T(8,128)(2,1)} %convolution_convert_fusion, f32[2048,2816]{1,0:T(8,128)} %fusion.67, bf16[1,2048,1024]{1,2,0:T(8,128)(2,1)} %copy, f32[2048]{0:T(1024)S(1)} %copy-done.18), kind=kOutput, calls=%fused_computation.61 | convolution fusion | flops 11852054528 | bytes 50339840 | tf_op jit(solution)/vmap(transpose(jvp()))/dot_general | solution.py:21
  384.7 0.5 copy-done.19
  385.2 0.6 dynamic-slice
  386.4 1.2 convert_bitcast_fusion.4
  387.6 1.2 convert_bitcast_fusion.3
  388.8 3.7 fusion.121
  392.7 59.9 %reduce-scatter.19.cloned.1.call-done = f32[1,64,2816]{2,1,0:T(8,128)} async-done(((f32[1,1024,2816]{2,1,0:T(8,128)}), f32[1,64,2816]{2,1,0:T(8,128)}) %reduce-scatter.19.cloned.1.call-update) | async-done | bytes 720912
  452.6 1.1 convert_bitcast_fusion.8
  453.7 88.6 %reduce-scatter.21.cloned.1.call-done = f32[1,64,2816]{2,1,0:T(8,128)} async-done(((f32[1,1024,2816]{2,1,0:T(8,128)}), f32[1,64,2816]{2,1,0:T(8,128)}) %reduce-scatter.21.cloned.1.call-update) | async-done | bytes 720912
  542.3 1.1 convert_bitcast_fusion.7
  543.5 4.6 fusion.123
  548.2 83.3 %reduce-scatter.23.cloned.1.call-done = f32[1,64,2816]{2,1,0:T(8,128)} async-done(((f32[1,1024,2816]{2,1,0:T(8,128)}), f32[1,64,2816]{2,1,0:T(8,128)}) %reduce-scatter.23.cloned.1.call-update) | async-done | bytes 720912
  631.5 1.1 convert_bitcast_fusion.6
  632.6 88.5 %reduce-scatter.25.cloned.1.call-done = f32[1,64,2816]{2,1,0:T(8,128)} async-done(((f32[1,1024,2816]{2,1,0:T(8,128)}), f32[1,64,2816]{2,1,0:T(8,128)}) %reduce-scatter.25.cloned.1.call-update) | async-done | bytes 720912
  721.2 1.1 convert_bitcast_fusion.5
  722.3 3.7 fusion.122
  726.1 75.7 %all-gather.14.cloned.1.call-done = bf16[1,2,2816,1024]{3,2,1,0:T(8,128)(2,1)} async-done(((bf16[1,2,176,1024]{3,2,1,0:T(8,128)(2,1)}), bf16[1,2,2816,1024]{3,2,1,0:T(8,128)(2,1)}) %all-gather.14.cloned.1.call-update) | async-done | bytes 11534352 | tf_op jit(solution)/reshape | solution.py:52
  801.9 81.8 %all-gather.10.cloned.1.call-done = bf16[1,2,1024,2816]{3,2,1,0:T(8,128)(2,1)} async-done(((bf16[1,2,64,2816]{3,2,1,0:T(8,128)(2,1)}), bf16[1,2,1024,2816]{3,2,1,0:T(8,128)(2,1)}) %all-gather.10.cloned.1.call-update) | async-done | bytes 11534352 | tf_op jit(solution)/reshape | solution.py:52
  883.7 81.8 %all-gather.12.cloned.1.call-done = bf16[1,2,1024,2816]{3,2,1,0:T(8,128)(2,1)} async-done(((bf16[1,2,64,2816]{3,2,1,0:T(8,128)(2,1)}), bf16[1,2,1024,2816]{3,2,1,0:T(8,128)(2,1)}) %all-gather.12.cloned.1.call-update) | async-done | bytes 11534352 | tf_op jit(solution)/reshape | solution.py:52
  965.5 11.7 %copy.5 = bf16[2,1024,2816]{2,1,0:T(8,128)(2,1)} copy(bf16[2,1024,2816]{2,1,0:T(8,128)(2,1)} %bitcast.332) | data formatting | bytes 23068672
  977.2 5.8 copy.6
  983.0 0.8 slice-done.1
  983.8 1.2 slice-done.2
  985.1 4.4 copy.7
  (64 shorter events, 1.2 us)
Async XLA Ops:
  7.2 379.2 %reduce-scatter.27.cloned.1.call-start = ((), (), s32[]{:S(2)}) async-start(), calls=%async_computation.13 | async-start | bytes 12255232
  16.8 20.0 %copy-start.17 = (f32[2048]{0:T(1024)}, f32[2048]{0:T(1024)S(1)}, u32[]{:S(2)}) copy-start(f32[2048]{0:T(1024)S(1)} %add_rsqrt_fusion) | copy-start | bytes 24580
  16.8 20.0 %copy-start.1 = (bf16[1,2048,1024]{2,1,0:T(8,128)(2,1)S(1)}, bf16[1,2048,1024]{2,1,0:T(8,128)(2,1)}, u32[]{:S(2)}) copy-start(bf16[1,2048,1024]{2,1,0:T(8,128)(2,1)} %param.2) | copy-start | bytes 12582916
  94.6 0.6 copy-start.13
  94.6 20.8 %copy-start.15 = (f32[1,1,2048]{2,1,0:T(1,128)}, f32[1,1,2048]{2,1,0:T(1,128)S(1)}, u32[]{:S(2)}) copy-start(f32[1,1,2048]{2,1,0:T(1,128)S(1)} %rsqrt.31) | copy-start | bytes 24580
  95.2 20.2 %copy-start.4 = (bf16[1,1,2048,1024]{2,3,1,0:T(8,128)(2,1)S(1)}, bf16[1,1,2048,1024]{2,3,1,0:T(8,128)(2,1)}, u32[]{:S(2)}) copy-start(bf16[1,1,2048,1024]{2,3,1,0:T(8,128)(2,1)} %get-tuple-element.10) | copy-start | bytes 12582916
  115.4 18.2 %copy-start.7 = (bf16[1,2048,1024]{2,1,0:T(8,128)(2,1)S(1)}, bf16[1,2048,1024]{2,1,0:T(8,128)(2,1)}, u32[]{:S(2)}) copy-start(bf16[1,2048,1024]{2,1,0:T(8,128)(2,1)} %param.5) | copy-start | bytes 12582916
  157.9 229.8 %reduce-scatter.29.cloned.1.call-start = ((), (), s32[]{:S(2)}) async-start(), calls=%async_computation.14 | async-start | bytes 12255232
  182.8 24.9 %copy-start.3 = (bf16[2048,2816]{1,0:T(8,128)(2,1)S(1)}, bf16[2048,2816]{1,0:T(8,128)(2,1)}, u32[]{:S(2)}) copy-start(bf16[2048,2816]{1,0:T(8,128)(2,1)} %convolution_convert_fusion.1) | copy-start | bytes 34603012
  228.2 20.8 %copy-start.14 = (f32[2048]{0:T(1024)S(1)}, f32[2048]{0:T(1024)}, u32[]{:S(2)}) copy-start(f32[2048]{0:T(1024)} %copy-done.13) | copy-start | bytes 24580
  228.2 20.8 %copy-start = (bf16[1,2048,1024]{1,2,0:T(8,128)(2,1)S(1)}, bf16[1,2048,1024]{1,2,0:T(8,128)(2,1)}, u32[]{:S(2)}) copy-start(bf16[1,2048,1024]{1,2,0:T(8,128)(2,1)} %copy.1) | copy-start | bytes 12582916
  228.2 20.8 %copy-start.5 = (bf16[1,1,2048,1024]{2,3,1,0:T(8,128)(2,1)S(1)}, bf16[1,1,2048,1024]{2,3,1,0:T(8,128)(2,1)}, u32[]{:S(2)}) copy-start(bf16[1,1,2048,1024]{2,3,1,0:T(8,128)(2,1)} %get-tuple-element.10) | copy-start | bytes 12582916
  228.2 20.8 %copy-start.16 = (f32[1,1,2048]{2,1,0:T(1,128)S(1)}, f32[1,1,2048]{2,1,0:T(1,128)}, u32[]{:S(2)}) copy-start(f32[1,1,2048]{2,1,0:T(1,128)} %copy-done.15) | copy-start | bytes 24580
  253.8 2.0 copy-start.6
  273.5 179.1 %reduce-scatter.19.cloned.1.call-start = ((), (), s32[]{:S(2)}) async-start(), calls=%async_computation.9 | async-start | bytes 12255232
  292.5 18.5 %copy-start.18 = (f32[2048]{0:T(1024)S(1)}, f32[2048]{0:T(1024)}, u32[]{:S(2)}) copy-start(f32[2048]{0:T(1024)} %copy-done.17) | copy-start | bytes 24580
  292.5 249.8 %reduce-scatter.21.cloned.1.call-start = ((), (), s32[]{:S(2)}) async-start(), calls=%async_computation.10 | async-start | bytes 12255232
  292.6 18.4 %copy-start.8 = (bf16[1,2048,1024]{1,2,0:T(8,128)(2,1)S(1)}, bf16[1,2048,1024]{1,2,0:T(8,128)(2,1)}, u32[]{:S(2)}) copy-start(bf16[1,2048,1024]{1,2,0:T(8,128)(2,1)} %copy) | copy-start | bytes 12582916
  337.1 294.3 %reduce-scatter.23.cloned.1.call-start = ((), (), s32[]{:S(2)}) async-start(), calls=%async_computation.11 | async-start | bytes 12255232
  360.8 360.4 %reduce-scatter.25.cloned.1.call-start = ((), (), s32[]{:S(2)}) async-start(), calls=%async_computation.12 | async-start | bytes 12255232
  384.5 0.7 copy-start.19
  384.5 4.3 copy-start.9
  384.5 4.3 copy-start.10
  384.6 417.3 %all-gather.14.cloned.1.call-start = ((), (), s32[]{:S(2)}) async-start(), calls=%async_computation.8 | async-start | bytes 12255232 | tf_op jit(solution)/reshape | solution.py:52
  392.6 329.8 %copy-start.11 = (f32[2,64,2816]{2,1,0:T(8,128)S(1)}, f32[2,64,2816]{2,1,0:T(8,128)}, u32[]{:S(2)}) copy-start(f32[2,64,2816]{2,1,0:T(8,128)} %param.8) | copy-start | bytes 4325380
  392.6 329.8 %copy-start.12 = (f32[2,64,2816]{2,1,0:T(8,128)S(1)}, f32[2,64,2816]{2,1,0:T(8,128)}, u32[]{:S(2)}) copy-start(f32[2,64,2816]{2,1,0:T(8,128)} %param.7) | copy-start | bytes 4325380
  392.6 491.1 %all-gather.10.cloned.1.call-start = ((), (), s32[]{:S(2)}) async-start(), calls=%async_computation.6 | async-start | bytes 12255232 | tf_op jit(solution)/reshape | solution.py:52
  548.1 417.4 %all-gather.12.cloned.1.call-start = ((), (), s32[]{:S(2)}) async-start(), calls=%async_computation.7 | async-start | bytes 12255232 | tf_op jit(solution)/reshape | solution.py:52
  965.5 11.7 %copy-start.2 = (bf16[1,2,1024,2816]{3,2,1,0:T(8,128)(2,1)S(1)}, bf16[1,2,1024,2816]{3,2,1,0:T(8,128)(2,1)}, u32[]{:S(2)}) copy-start(bf16[1,2,1024,2816]{3,2,1,0:T(8,128)(2,1)} %all-gather.12.cloned.1.call-done) | copy-start | bytes 34603012
  965.5 17.5 %slice-start = ((s8[11534336]{0:T(1024)(128)(4,1)}), s8[4194304]{0:T(1024)(128)(4,1)S(1)}, s32[]{:S(2)}) async-start(s8[11534336]{0:T(1024)(128)(4,1)} %bitcast.329), calls=%async_computation.15 | async-start | bytes 8388608
  965.5 18.3 %slice-start.1 = ((s8[11534336]{0:T(1024)(128)(4,1)}), s8[4194304]{0:T(1024)(128)(4,1)S(1)}, s32[]{:S(2)}) async-start(s8[11534336]{0:T(1024)(128)(4,1)} %bitcast.329), calls=%async_computation.16 | async-start | bytes 8388608
  977.2 7.9 slice-start.2
Sparse Core Ops, SparseCore 0:
  158.0 89.4 reduce-scatter.26
  273.6 89.4 reduce-scatter.28
  366.3 86.1 reduce-scatter.18
  456.3 85.9 reduce-scatter.20
  545.5 85.9 reduce-scatter.22
  635.2 85.9 reduce-scatter.24
  723.1 78.6 all-gather.13
  804.4 79.2 all-gather.9
  886.2 79.2 all-gather.11
where the time goes:
time: 1000 us; the launch traced here: 996 us
  waiting for transfers between devices  560 us (56%)
  matrix products  308 us (31%)
  other arithmetic  69.8 us (7%)
  local copies, waits for them, and re-layouts  42.4 us (4%)
  between operations  15.2 us (2%)
    unnamed x15, waiting for transfers between devices  321 us
    reshape x3, waiting for transfers between devices, step(): t.reshape(-1, *t.shape[2:])  239 us
    dot_general x5, matrix products, layer(): gate = jnp.dot(a, w['w_gate'], preferred_element_type=jnp.float32)  106 us
    dot_general x5, matrix products, layer(): up = jnp.dot(a, w['w_up'], preferred_element_type=jnp.float32)  104 us
    dot_general x5, matrix products, matmul(): jnp.dot(a, w, preferred_element_type=jnp.float32).astype(jnp.bfloat16)  98.2 us
    unnamed x4, other arithmetic  47.8 us
    unnamed x51, local copies, waits for them, and re-layouts  41.8 us
  transfers between devices with their start and end apart: 9, of which 7 were waited for; matrix products, arithmetic and copies ran while one was open for 24% of the time, Pallas kernels for 0%

commit v1 on v0

v1 whole, which is shorter than its diff:
```python
import functools
import math

import jax
import jax.numpy as jnp
from jax import lax
from jax.experimental import pallas as pl
from jax.experimental.pallas import tpu as pltpu
from jax.sharding import PartitionSpec as P

BF, F32 = jnp.bfloat16, jnp.float32
MESH = pl.DeviceIdType.MESH
TILE = 256


def dot(a, b, dims):
    return lax.dot_general(a, b, (dims, ((), ())), preferred_element_type=F32)


def normed(h):
    wide = h.astype(F32)
    scale = lax.rsqrt(jnp.mean(wide**2, -1, keepdims=True) + 1e-6)
    return (wide * scale).astype(BF), scale


def normed_back(h, scale, da):
    wide, da = h.astype(F32), da.astype(F32)
    inner = jnp.mean(wide * da, -1, keepdims=True)
    return (scale * (da - wide * (scale * scale * inner))).astype(BF)


def gate_up(a, wg, wu):
    return dot(a, wg, ((1,), (0,))), dot(a, wu, ((1,), (0,)))


def back(a, gate, up, hid, dy, wg, wu, wd, deeper):
    d_wd = dot(hid, dy, ((0,), (0,))).astype(BF)
    d_hid = dot(dy, wd, ((1,), (1,))).astype(BF).astype(F32)
    sig = jax.nn.sigmoid(gate)
    d_up = (d_hid * (gate * sig)).astype(BF)
    d_gate = (d_hid * up * (sig * (1 + gate * (1 - sig)))).astype(BF)
    d_wg = dot(a, d_gate, ((0,), (0,))).astype(BF)
    d_wu = dot(a, d_up, ((0,), (0,))).astype(BF)
    da = None
    if deeper:
        da = dot(d_gate, wg, ((1,), (1,))).astype(BF) + dot(d_up, wu, ((1,), (1,))).astype(BF)
    return d_wg, d_wu, d_wd, da


class Flow:
    pass


def sync_kernel(side, tiles, *refs):
    (dwg, dwu, dwd, wg, wu, wd, mg, mu, md, vg, vu, vd,
     og, ou, od, omg, omu, omd, ovg, ovu, ovd,
     L, R1, R2, MV, W, NW, D, R1d, R2d, MVd, Wd, NWd,
     ss, rs, ssd, rsd, ls, lsd, ld, ldd) = refs
    rep, me = lax.axis_index("rep"), lax.axis_index("dp")
    x, y = me // side, me % side

    def mod(v):
        return (v + 2 * side) % side

    def at(xx, yy):
        return (rep, mod(xx) * side + mod(yy))

    barrier = pltpu.get_barrier_semaphore()
    for dx, dy in ((1, 0), (-1, 0), (0, 1), (0, -1)):
        pl.semaphore_signal(barrier, inc=1, device_id=at(x + dx, y + dy), device_id_type=MESH)
    pl.semaphore_wait(barrier, 4)

    slots = tiles

    def tile_of(c, t):
        g = 2 * t + c // 2
        layer = 1 - g // tiles
        return layer, pl.multiple_of((g % tiles) * TILE, TILE)

    gu = Flow()
    gu.local = lambda c, t: L.at[t % 3, c]
    gu.r1 = lambda c, t, s: R1.at[t % 2, c, s]
    gu.r2 = lambda c, t, s: R2.at[t % 2, c, s]
    gu.nw = lambda c, t: NW.at[t % 2, c]
    gu.sems = lambda c, t, k: (ss.at[t % 2, c, k], rs.at[t % 2, c, k])
    gu.mv = lambda c, t: (MV.at[c, 0], MV.at[c, 1])
    gu.w = lambda c, t: W.at[c]
    gu.ls = lambda c, t, k: ls.at[c, k]

    def gu_out(c, t):
        layer, j = tile_of(c, t)
        return (og, ou)[c % 2].at[layer, :, :, :, pl.ds(j, TILE)]

    def gu_hbm(c, t):
        layer, j = tile_of(c, t)
        kind = c % 2
        cut = (layer, slice(None), pl.ds(j, TILE))
        return ((mg, mu)[kind].at[cut], (vg, vu)[kind].at[cut], (wg, wu)[kind].at[layer, x, y, :, pl.ds(j, TILE)],
                (omg, omu)[kind].at[cut], (ovg, ovu)[kind].at[cut])

    gu.out, gu.hbm = gu_out, gu_hbm

    def down(ab):
        fl = Flow()
        lane = lambda c: pl.ds(128 * (4 * ab + c), 128)
        fl.local = lambda c, t: D.at[t, :, :, :, lane(c)]
        fl.r1 = lambda c, t, s: R1d.at[ab, c, s]
        fl.r2 = lambda c, t, s: R2d.at[ab, c, s]
        fl.nw = lambda c, t: NWd.at[ab, c]
        fl.sems = lambda c, t, k: (ssd.at[ab, c, k], rsd.at[ab, c, k])
        fl.mv = lambda c, t: (MVd.at[ab, c, 0], MVd.at[ab, c, 1])
        fl.w = lambda c, t: Wd.at[ab, c]
        fl.ls = lambda c, t, k: lsd.at[ab, c, k]
        fl.out = lambda c, t: od.at[t, :, :, :, lane(c)]

        def hbm(c, t):
            cut = (t, slice(None), lane(c))
            return md.at[cut], vd.at[cut], wd.at[t, x, y, :, lane(c)], omd.at[cut], ovd.at[cut]

        fl.hbm = hbm
        return fl

    downs = (down(0), down(1))

    def stage(fl, c, t, k):
        first, sg = c < 2, (1, -1)[c % 2]
        p1, p2 = (x, y) if first else (y, x)
        along = (at(x + sg, y), at(x, y + sg))
        nb1, nb2 = along if first else along[::-1]
        loc = fl.local(c, t)

        def chunk(ref, q):
            return ref.at[q] if first else ref.at[:, q]

        def sub(ref, q, q2):
            return ref.at[q, q2] if first else ref.at[q2, q]

        def copy(k):
            send, recv = fl.sems(c, t, k)
            if k < 3:
                src, dst, to = chunk(loc, mod(p1 - sg * (1 + k))), fl.r1(c, t, k), nb1
            elif k < 6:
                src, dst, to = sub(loc, p1, mod(p2 - sg * (k - 2))), fl.r2(c, t, k - 3), nb2
            elif k < 9:
                dst, to = sub(fl.out(c, t), p1, mod(p2 - sg * (k - 6))), nb2
                src = fl.nw(c, t) if k == 6 else dst
            else:
                dst, to = chunk(fl.out(c, t), mod(p1 - sg * (k - 9))), nb1
                src = dst
            return pltpu.make_async_remote_copy(src, dst, send, recv, device_id=to, device_id_type=MESH)

        def locals_(ins_too):
            hm, hv, hw, hom, hov = fl.hbm(c, t)
            bm, bv = fl.mv(c, t)
            own = sub(fl.out(c, t), p1, p2)
            s = lambda n: fl.ls(c, t, n)
            if ins_too:
                return [pltpu.make_async_copy(a, b, s(n)) for n, (a, b) in enumerate(((hm, bm), (hv, bv), (hw, fl.w(c, t))))]
            return [pltpu.make_async_copy(a, b, s(3 + n)) for n, (a, b) in enumerate(((bm, hom), (bv, hov), (fl.nw(c, t), own)))]

        if k > 0:
            copy(k - 1).wait()
        if k in (1, 2):
            mine = chunk(loc, mod(p1 - sg * (1 + k)))
            mine[...] = (mine[...].astype(F32) + fl.r1(c, t, k - 1)[...].astype(F32)).astype(BF)
        elif k in (3, 4, 5):
            q2 = mod(p2 - sg * (k - 2))
            mine = sub(loc, p1, q2)
            total = mine[...].astype(F32) + fl.r1(c, t, 2).at[q2][...].astype(F32)
            if k > 3:
                total += fl.r2(c, t, k - 4)[...].astype(F32)
            mine[...] = total.astype(BF)
            if k == 3:
                for one in locals_(True):
                    one.start()
        elif k == 6:
            total = sub(loc, p1, p2)[...].astype(F32) + fl.r1(c, t, 2).at[p2][...].astype(F32)
            g = (total + fl.r2(c, t, 2)[...].astype(F32)).astype(BF).astype(F32)
            for one in locals_(True):
                one.wait()
            bm, bv = fl.mv(c, t)
            m = 0.9 * bm[...] + 0.1 * g
            v = 0.95 * bv[...] + 0.05 * g * g
            w = fl.w(c, t)[...].astype(F32)
            bm[...] = m
            bv[...] = v
            fl.nw(c, t)[...] = (w - 0.02 * (m * lax.rsqrt(v + 1e-8) + 0.1 * w)).astype(BF)
            for one in locals_(False):
                one.start()
        elif k == 7:
            for one in locals_(False):
                one.wait()
        if k < 12:
            copy(k).start()

    def load(c, t):
        layer, j = tile_of(c, t)
        return pltpu.make_async_copy((dwg, dwu)[c % 2].at[layer, :, :, :, pl.ds(j, TILE)], L.at[t % 3, c], ld.at[t % 2, c])

    for layer in (0, 1):
        pltpu.make_async_copy(dwd.at[layer], D.at[layer], ldd.at[layer]).start()

    def round_(i, rho):
        for k in range(12, -1, -1):
            for pair in (0, 1):
                off = 2 + 2 * pair
                if (k + off) % 4 == rho:
                    t = i - (k + off) // 4

                    @pl.when((t >= 0) & (t < slots))
                    def _():
                        for c in (2 * pair, 2 * pair + 1):
                            if k == 0:
                                load(c, t).wait()
                            stage(gu, c, t, k)
            for ab in (0, 1):
                off = 2 * ab
                if (k + off) % 4 == rho:
                    i0 = i - (k + off) // 4
                    a, b = (tiles + 1) // 2, tiles

                    @pl.when((i0 == a) | (i0 == b))
                    def _():
                        layer = jnp.where(i0 == a, 1, 0)
                        if k == 0 and ab == 0:
                            pltpu.make_async_copy(dwd.at[layer], D.at[layer], ldd.at[layer]).wait()
                        for c in range(4):
                            stage(downs[ab], c, layer, k)

    def turn(i, carry):
        @pl.when(i < slots)
        def _():
            for c in range(4):
                load(c, i).start()

        for rho in range(4):
            round_(i, rho)
        return carry

    lax.fori_loop(0, slots + 4, turn, 0)


def synced(mesh, d_ws, ws, ms, vs):
    n = mesh.shape["dp"]
    side = math.isqrt(n)
    layers, d, ff = ws[0].shape
    tiles = ff // TILE
    cut = lambda a: a.reshape(layers, side, side, a.shape[1] // n, a.shape[2])
    rows, rowsd = d // n, ff // n
    hbm = pl.BlockSpec(memory_space=pl.ANY)
    ws5 = [cut(w) for w in ws]
    out_shape = [jax.ShapeDtypeStruct(w.shape, BF) for w in ws5] + [jax.ShapeDtypeStruct(m.shape, F32) for m in (*ms, *vs)]
    gu, dn = (rows, TILE), (rowsd, 128)
    dma = pltpu.SemaphoreType.DMA
    scratch = [
        pltpu.VMEM((3, 4, side, side, *gu), BF),
        pltpu.VMEM((2, 4, 3, side, *gu), BF),
        pltpu.VMEM((2, 4, 3, *gu), BF),
        pltpu.VMEM((4, 2, *gu), F32),
        pltpu.VMEM((4, *gu), BF),
        pltpu.VMEM((2, 4, *gu), BF),
        pltpu.VMEM((layers, side, side, rowsd, d), BF),
        pltpu.VMEM((2, 4, 3, side, *dn), BF),
        pltpu.VMEM((2, 4, 3, *dn), BF),
        pltpu.VMEM((2, 4, 2, *dn), F32),
        pltpu.VMEM((2, 4, *dn), BF),
        pltpu.VMEM((2, 4, *dn), BF),
        dma((2, 4, 12)), dma((2, 4, 12)), dma((2, 4, 12)), dma((2, 4, 12)),
        dma((4, 6)), dma((2, 4, 6)), dma((2, 4)), dma((2,)),
    ]
    res = pl.pallas_call(
        functools.partial(sync_kernel, side, tiles),
        out_shape=out_shape,
        in_specs=[hbm] * 12,
        out_specs=[hbm] * 9,
        scratch_shapes=scratch,
        compiler_params=pltpu.CompilerParams(collective_id=0, has_side_effects=True, vmem_limit_bytes=60 * 2**20),
        name="sync",
    )(*(cut(g) for g in d_ws), *ws5, *ms, *vs)
    return [r.reshape(w.shape) for r, w in zip(res[:3], ws)] + list(res[3:])


def solution(mesh):
    def step(x, dy, wg, wu, wd, *mv):
        x, dy = x[0], dy[0]
        a0, s0 = normed(x)
        g0, u0 = gate_up(a0, wg[0], wu[0])
        hid0 = (jax.nn.silu(g0) * u0).astype(BF)
        h1 = x + dot(hid0, wd[0], ((1,), (0,))).astype(BF)
        a1, s1 = normed(h1)
        g1, u1 = gate_up(a1, wg[1], wu[1])
        hid1 = (jax.nn.silu(g1) * u1).astype(BF)
        d_wg1, d_wu1, d_wd1, da = back(a1, g1, u1, hid1, dy, wg[1], wu[1], wd[1], True)
        dh1 = dy + normed_back(h1, s1, da)
        d_wg0, d_wu0, d_wd0, _ = back(a0, g0, u0, hid0, dh1, wg[0], wu[0], wd[0], False)
        grads = [jnp.stack(p) for p in ((d_wg0, d_wg1), (d_wu0, d_wu1), (d_wd0, d_wd1))]
        return tuple(synced(mesh, grads, (wg, wu, wd), mv[:3], mv[3:]))

    rd, rep, shard = P(("rep", "dp")), P(), P(None, "dp", None)
    out, outs = P("rep"), P("rep", "dp", None)
    return jax.shard_map(
        step,
        mesh=mesh,
        in_specs=(rd, rd, rep, rep, rep, *[shard] * 6),
        out_specs=(out, out, out, *[outs] * 6),
        check_vma=False,
    )
```

time: 1000 us -> 808 us (0.81)
  waiting for transfers between devices: 560 us -> 0 us
  Pallas kernels: 0 us -> 410 us
  other arithmetic: 69.8 us -> 27.8 us
  between operations: 15.2 us -> 1.3 us
    pallas_call x0 -> x1, Pallas kernels: none -> 410 us  [synced(): pl.pallas_call(functools.partial(sync_kernel, side, tiles), out_shape=out...]
    unnamed x15 -> x0, waiting for transfers between devices: 321 us -> none
    reshape x3 -> x0, waiting for transfers between devices: 239 us -> none  [step(): t.reshape(-1, *t.shape[2:])]
    unnamed x4 -> x1, other arithmetic: 47.8 us -> 0.01 us
    another operation x0 -> x2, other arithmetic: none -> 18.1 us  [step(): jnp.stack(p)]
    reshape x3 -> x0, other arithmetic: 12 us -> none  [step(): t.reshape(-1, *t.shape[2:])]
    unnamed x51 -> x55, local copies, waits for them, and re-layouts: 41.8 us -> 44.6 us
  transfers between devices with their start and end apart: 9 -> 0, of which waited for: 7 -> 0; matrix products, arithmetic and copies ran while one was open for 24% -> 0% of each run, Pallas kernels for 0% -> 0%
where the time goes in v1:
time: 808 us; the launch traced here: 801 us
  Pallas kernels  410 us (51%)
  matrix products  317 us (39%)
  local copies, waits for them, and re-layouts  44.6 us (6%)
  other arithmetic  27.8 us (3%)
    pallas_call x1, Pallas kernels, synced(): pl.pallas_call(functools.partial(sync_kernel, side, tiles), out_shape=out...  410 us
    dot_general x15, matrix products, dot(): return lax.dot_general(a, b, (dims, ((), ())), preferred_element_type=F32)  317 us
    unnamed x55, local copies, waits for them, and re-layouts  44.6 us
    another operation x2, other arithmetic, step(): jnp.stack(p)  18.1 us

profile of v1, /device:TPU:96, one launch (start us, length us, event | category | flops | bytes accessed | tf_op | source)
XLA Modules:
  0.0 801.5 jit_solution(8078974646689085854)
XLA Ops:
  0.6 6.5 copy.20
  7.2 3.1 fusion.13
  10.2 0.0 copy-start.17
  10.2 19.9 %fusion.34 = f32[2048,2816]{1,0:T(8,128)} fusion(bf16[2,1024,2816]{2,1,0:T(8,128)(2,1)} %param.13, bf16[1,2048,1024]{2,1,0:T(8,128)(2,1)} %param.11, f32[2048]{0:T(1024)S(1)} %add_rsqrt_fusion.1), kind=kOutput, calls=%fused_computation.53 | convolution fusion | flops 11817451520 | bytes 33038336 | tf_op jit(solution)/shard_map/dot_general | solution.py:17
  30.1 0.0 copy-done.17
  30.1 28.7 %multiply_convert_fusion.1 = (bf16[2048,2816]{1,0:T(8,128)(2,1)}, f32[2048,2816]{1,0:T(8,128)}) fusion(f32[2048,2816]{1,0:T(8,128)} %fusion.34, bf16[2,1024,2816]{2,1,0:T(8,128)(2,1)} %param.14, bf16[1,2048,1024]{2,1,0:T(8,128)(2,1)} %param.11, f32[2048]{0:T(1024)S(1)} %add_rsqrt_fusion.1), kind=kOutput, calls=%fused_computation.13 | convolution fusion | flops 11852054528 | bytes 67641344 | tf_op jit(solution)/shard_map/dot_general | solution.py:17
  58.8 19.5 %fusion.17 = (f32[2048]{0:T(1024)S(1)}, bf16[2048,1024]{0,1:T(8,128)(2,1)}) fusion(bf16[2048,2816]{1,0:T(8,128)(2,1)} %get-tuple-element.29, bf16[2,2816,1024]{2,1,0:T(8,128)(2,1)} %param.15, bf16[1,2048,1024]{1,2,0:T(8,128)(2,1)} %copy.20), kind=kOutput, calls=%fused_computation.35 | convolution fusion | flops 11821643776 | bytes 25698304 | tf_op jit(solution)/shard_map/dot_general | solution.py:17
  78.3 0.0 copy-start.13
  78.4 0.0 copy-start.5
  78.4 20.3 %fusion.26 = f32[2048,2816]{1,0:T(8,128)} fusion(bf16[2,1024,2816]{2,1,0:T(8,128)(2,1)} %param.14, bf16[2048,1024]{0,1:T(8,128)(2,1)} %get-tuple-element.32, f32[2048]{0:T(1024)S(1)} %add_rsqrt_fusion), kind=kOutput, calls=%fused_computation.45 | convolution fusion | flops 11817451520 | bytes 33038336 | tf_op jit(solution)/shard_map/dot_general | solution.py:17
  98.6 0.0 copy-done.15
  98.6 0.0 copy-done.5
  98.6 18.1 %fusion.22 = f32[2048,2816]{1,0:T(8,128)} fusion(bf16[2,1024,2816]{2,1,0:T(8,128)(2,1)} %param.13, bf16[2048,1024]{0,1:T(8,128)(2,1)S(1)} %copy-done.5, f32[2048]{0:T(1024)S(1)} %add_rsqrt_fusion), kind=kOutput, calls=%fused_computation.41 | convolution fusion | flops 11817451520 | bytes 33038336 | tf_op jit(solution)/shard_map/dot_general | solution.py:17
  116.7 33.9 %fusion.2 = (bf16[2048,2816]{1,0:T(8,128)(2,1)}, bf16[2048,2816]{1,0:T(8,128)(2,1)}) fusion(f32[2048,2816]{1,0:T(8,128)} %fusion.22, f32[2048,2816]{1,0:T(8,128)} %fusion.26, bf16[2,2816,1024]{2,1,0:T(8,128)(2,1)} %param.15, bf16[1,2048,1024]{2,1,0:T(8,128)(2,1)} %param.12), kind=kOutput, calls=%fused_computation.6 | convolution fusion | flops 11897667584 | bytes 79167488 | tf_op jit(solution)/shard_map/dot_general | solution.py:17
  150.6 16.8 %fusion.20 = bf16[2048,1024]{0,1:T(8,128)(2,1)S(1)} fusion(bf16[2048,2816]{1,0:T(8,128)(2,1)} %get-tuple-element.28, bf16[2,1024,2816]{2,1,0:T(8,128)(2,1)} %param.13), kind=kOutput, calls=%fused_computation.39 | convolution fusion | flops 11811160064 | bytes 21495808 | tf_op jit(solution)/shard_map/dot_general | solution.py:17
  167.4 0.0 copy-done.6
  167.4 0.0 copy-start.16
  167.4 18.4 %fusion.19 = (f32[2048]{0:T(1024)S(1)}, bf16[2048,1024]{0,1:T(8,128)(2,1)}) fusion(bf16[2048,1024]{0,1:T(8,128)(2,1)S(1)} %copy-done.6, bf16[2048,1024]{0,1:T(8,128)(2,1)S(1)} %fusion.20, bf16[2048,2816]{1,0:T(8,128)(2,1)} %get-tuple-element.27, bf16[2,1024,2816]{2,1,0:T(8,128)(2,1)} %param.14), kind=kOutput, calls=%fused_computation.37 | convolution fusion | flops 11823740928 | bytes 29892608 | tf_op jit(solution)/shard_map/dot_general | solution.py:17
  185.8 0.0 copy-done.16
  185.9 6.5 copy.21
  192.4 6.7 fusion.53
  199.1 17.0 %convolution_convert_fusion.2 = bf16[2816,1024]{1,0:T(8,128)(2,1)} fusion(bf16[2048,2816]{1,0:T(8,128)(2,1)} %get-tuple-element.29, bf16[2048,1024]{0,1:T(8,128)(2,1)S(1)} %fusion.53), kind=kOutput, calls=%fused_computation.61 | convolution fusion | flops 11814043648 | bytes 21495808 | tf_op jit(solution)/shard_map/dot_general | solution.py:17
  216.0 23.8 %fusion.39 = bf16[2816,1024]{1,0:T(8,128)(2,1)} fusion(f32[2048,2816]{1,0:T(8,128)} %fusion.26, bf16[1,2048,1024]{2,1,0:T(8,128)(2,1)} %param.12, f32[2048,2816]{1,0:T(8,128)} %fusion.22), kind=kOutput, calls=%fused_computation.58 | convolution fusion | flops 11848646656 | bytes 56098816 | tf_op jit(solution)/shard_map/dot_general | solution.py:17
  239.8 9.7 %pad_maximum_fusion.2.refs_2_ = bf16[2,4,4,176,1024]{4,3,2,1,0:T(8,128)(2,1)} fusion(bf16[1,4,4,176,1024]{4,3,2,1,0:T(8,128)(2,1)} %bitcast.91, bf16[1,4,4,176,1024]{4,3,2,1,0:T(8,128)(2,1)} %bitcast.90), kind=kLoop, calls=%fused_computation.24 | loop fusion | flops 5767168 | bytes 23068672 | tf_op jit(solution)/shard_map/stack | solution.py:296
  249.4 17.2 %convolution_convert_fusion = bf16[2048,2816]{1,0:T(8,128)(2,1)} fusion(bf16[2048,1024]{0,1:T(8,128)(2,1)S(1)} %fusion.53, bf16[2,2816,1024]{2,1,0:T(8,128)(2,1)} %param.15), kind=kOutput, calls=%fused_computation.26 | convolution fusion | flops 11816927232 | bytes 21495808 | tf_op jit(solution)/shard_map/dot_general | solution.py:17
  266.7 23.0 %fusion.43 = bf16[1024,2816]{1,0:T(8,128)(2,1)} fusion(bf16[2048,2816]{1,0:T(8,128)(2,1)} %convolution_convert_fusion, f32[2048,2816]{1,0:T(8,128)} %fusion.34, bf16[1,2048,1024]{1,2,0:T(8,128)(2,1)} %copy.20, f32[2048]{0:T(1024)S(1)} %copy-done.18), kind=kOutput, calls=%fused_computation.60 | convolution fusion | flops 11860705280 | bytes 44572672 | tf_op jit(solution)/shard_map/dot_general | solution.py:17
  289.7 18.7 %convolution_convert_fusion.3 = bf16[1024,2816]{1,0:T(8,128)(2,1)} fusion(bf16[2048,2816]{1,0:T(8,128)(2,1)} %get-tuple-element.27, bf16[2048,1024]{0,1:T(8,128)(2,1)} %get-tuple-element.32, f32[2048]{0:T(1024)S(1)} %copy-done.14), kind=kOutput, calls=%fused_computation.62 | convolution fusion | flops 11820335104 | bytes 21504000 | tf_op jit(solution)/shard_map/dot_general | solution.py:17
  308.4 0.0 copy-done
  308.4 24.9 %fusion.40 = bf16[1024,2816]{1,0:T(8,128)(2,1)} fusion(f32[2048,2816]{1,0:T(8,128)} %get-tuple-element.30, bf16[2048,2816]{1,0:T(8,128)(2,1)} %convolution_convert_fusion, f32[2048,2816]{1,0:T(8,128)} %fusion.34, bf16[1,2048,1024]{1,2,0:T(8,128)(2,1)S(1)} %copy-done, f32[2048]{0:T(1024)S(1)} %copy-done.18), kind=kOutput, calls=%fused_computation.59 | convolution fusion | flops 11883773952 | bytes 67641344 | tf_op jit(solution)/shard_map/dot_general | solution.py:17
  333.3 17.2 %convolution_convert_fusion.4 = bf16[1024,2816]{1,0:T(8,128)(2,1)S(1)} fusion(bf16[2048,2816]{1,0:T(8,128)(2,1)} %get-tuple-element.28, bf16[2048,1024]{0,1:T(8,128)(2,1)} %get-tuple-element.32, f32[2048]{0:T(1024)S(1)} %copy-done.14), kind=kOutput, calls=%fused_computation.63 | convolution fusion | flops 11820335104 | bytes 21504000 | tf_op jit(solution)/shard_map/dot_general | solution.py:17
  350.5 8.4 %pad_maximum_fusion = (bf16[2,4,4,64,2816]{4,3,2,1,0:T(8,128)(2,1)}, bf16[2,4,4,64,2816]{4,3,2,1,0:T(8,128)(2,1)}) fusion(bf16[1,4,4,64,2816]{4,3,2,1,0:T(8,128)(2,1)S(1)} %bitcast.89, bf16[1,4,4,64,2816]{4,3,2,1,0:T(8,128)(2,1)S(1)} %bitcast.88, bf16[1,4,4,64,2816]{4,3,2,1,0:T(8,128)(2,1)S(1)} %bitcast.87, bf16[1,4,4,64,2816]{4,3,2,1,0:T(8,128)(2,1)S(1)} %bitcast.86), kind=kLoop, calls=%fused_computation.22 | loop fusion | flops 11534336 | bytes 46137344 | tf_op jit(solution)/shard_map/stack | solution.py:296
  359.0 410.4 %sync.1 = (bf16[2,4,4,64,2816]{4,3,2,1,0:T(8,128)(2,1)}, bf16[2,4,4,64,2816]{4,3,2,1,0:T(8,128)(2,1)}, bf16[2,4,4,176,1024]{4,3,2,1,0:T(8,128)(2,1)}, f32[2,64,2...) custom-call(bf16[2,4,4,64,2816]{4,3,2,1,0:T(8,128)(2,1)} %get-tuple-, ...), custom_call_target="tpu_custom_call" | custom-call | tf_op jit(solution)/shard_map/sync/pallas_call | solution.py:271
  769.4 0.0 slice-start
  769.4 0.0 slice-start.1
  769.4 11.7 %copy.31 = bf16[2,1024,2816]{2,1,0:T(8,128)(2,1)} copy(bf16[2,1024,2816]{2,1,0:T(8,128)(2,1)} %bitcast.85) | data formatting | bytes 23068672
  781.1 0.0 copy-done.1
  781.1 5.8 copy.32
  787.0 0.7 slice-done.1
  787.6 1.3 slice-done.2
  789.0 5.4 copy.33
  794.3 0.0 copy-done.12
  794.3 1.1 copy.34
  795.5 1.1 copy.35
  796.6 0.0 copy-done.10
  796.6 1.1 copy.36
  797.7 1.1 copy.37
  798.8 1.1 copy.38
  799.9 1.1 copy.39
  (31 shorter events, 0.1 us)
Async XLA Ops:
  10.2 19.9 %copy-start.17 = (f32[2048]{0:T(1024)}, f32[2048]{0:T(1024)S(1)}, u32[]{:S(2)}) copy-start(f32[2048]{0:T(1024)S(1)} %add_rsqrt_fusion.1) | copy-start | bytes 24580
  78.3 20.3 %copy-start.15 = (f32[2048]{0:T(1024)}, f32[2048]{0:T(1024)S(1)}, u32[]{:S(2)}) copy-start(f32[2048]{0:T(1024)S(1)} %get-tuple-element.31) | copy-start | bytes 24580
  78.3 114.0 %copy-start.13 = (f32[2048]{0:T(1024)}, f32[2048]{0:T(1024)S(1)}, u32[]{:S(2)}) copy-start(f32[2048]{0:T(1024)S(1)} %add_rsqrt_fusion) | copy-start | bytes 24580
  78.4 20.3 %copy-start.5 = (bf16[2048,1024]{0,1:T(8,128)(2,1)S(1)}, bf16[2048,1024]{0,1:T(8,128)(2,1)}, u32[]{:S(2)}) copy-start(bf16[2048,1024]{0,1:T(8,128)(2,1)} %get-tuple-element.32) | copy-start | bytes 12582916
  150.6 16.8 %copy-start.6 = (bf16[2048,1024]{0,1:T(8,128)(2,1)S(1)}, bf16[2048,1024]{0,1:T(8,128)(2,1)}, u32[]{:S(2)}) copy-start(bf16[2048,1024]{0,1:T(8,128)(2,1)} %get-tuple-element.32) | copy-start | bytes 12582916
  167.4 18.4 %copy-start.16 = (f32[2048]{0:T(1024)S(1)}, f32[2048]{0:T(1024)}, u32[]{:S(2)}) copy-start(f32[2048]{0:T(1024)} %copy-done.15) | copy-start | bytes 24580
  249.4 17.3 %copy-start.18 = (f32[2048]{0:T(1024)S(1)}, f32[2048]{0:T(1024)}, u32[]{:S(2)}) copy-start(f32[2048]{0:T(1024)} %copy-done.17) | copy-start | bytes 24580
  266.7 23.0 %copy-start.14 = (f32[2048]{0:T(1024)S(1)}, f32[2048]{0:T(1024)}, u32[]{:S(2)}) copy-start(f32[2048]{0:T(1024)} %copy-done.13) | copy-start | bytes 24580
  289.7 18.7 %copy-start = (bf16[1,2048,1024]{1,2,0:T(8,128)(2,1)S(1)}, bf16[1,2048,1024]{1,2,0:T(8,128)(2,1)}, u32[]{:S(2)}) copy-start(bf16[1,2048,1024]{1,2,0:T(8,128)(2,1)} %copy.20) | copy-start | bytes 12582916
  333.3 17.2 %copy-start.2 = (bf16[1024,2816]{1,0:T(8,128)(2,1)S(1)}, bf16[1024,2816]{1,0:T(8,128)(2,1)}, u32[]{:S(2)}) copy-start(bf16[1024,2816]{1,0:T(8,128)(2,1)} %fusion.43) | copy-start | bytes 17301508
  333.3 17.2 %copy-start.3 = (bf16[1024,2816]{1,0:T(8,128)(2,1)S(1)}, bf16[1024,2816]{1,0:T(8,128)(2,1)}, u32[]{:S(2)}) copy-start(bf16[1024,2816]{1,0:T(8,128)(2,1)} %convolution_convert_fusion.3) | copy-start | bytes 17301508
  333.3 17.2 %copy-start.4 = (bf16[1024,2816]{1,0:T(8,128)(2,1)S(1)}, bf16[1024,2816]{1,0:T(8,128)(2,1)}, u32[]{:S(2)}) copy-start(bf16[1024,2816]{1,0:T(8,128)(2,1)} %fusion.40) | copy-start | bytes 17301508
  769.4 11.7 %copy-start.1 = (bf16[2,4,4,64,2816]{4,3,2,1,0:T(8,128)(2,1)S(1)}, bf16[2,4,4,64,2816]{4,3,2,1,0:T(8,128)(2,1)}, u32[]{:S(2)}) copy-start(bf16[2,4,4,64,2816]{4,3,2,1,0:T(8,128)(2,1)} %get-tuple-element.19) | copy-start | bytes 34603012
  769.4 17.6 %slice-start = ((s8[11534336]{0:T(1024)(128)(4,1)}), s8[4194304]{0:T(1024)(128)(4,1)S(1)}, s32[]{:S(2)}) async-start(s8[11534336]{0:T(1024)(128)(4,1)} %bitcast.81), calls=%async_computation | async-start | bytes 8388608
  769.4 18.2 %slice-start.1 = ((s8[11534336]{0:T(1024)(128)(4,1)}), s8[4194304]{0:T(1024)(128)(4,1)S(1)}, s32[]{:S(2)}) async-start(s8[11534336]{0:T(1024)(128)(4,1)} %bitcast.81), calls=%async_computation.1 | async-start | bytes 8388608
  781.1 7.8 slice-start.2
  789.0 5.4 copy-start.12
  789.0 6.5 copy-start.11
  789.0 7.6 copy-start.10
  794.3 3.3 copy-start.9
  794.3 4.4 copy-start.8
  794.3 5.5 copy-start.7

commit v2 on v1

--- a/solution.py
+++ b/solution.py
@@ -23,39 +23,21 @@
     return (wide * scale).astype(BF), scale
 
 
-def normed_back(h, scale, da):
-    wide, da = h.astype(F32), da.astype(F32)
-    inner = jnp.mean(wide * da, -1, keepdims=True)
-    return (scale * (da - wide * (scale * scale * inner))).astype(BF)
-
-
 def gate_up(a, wg, wu):
     return dot(a, wg, ((1,), (0,))), dot(a, wu, ((1,), (0,)))
 
 
-def back(a, gate, up, hid, dy, wg, wu, wd, deeper):
-    d_wd = dot(hid, dy, ((0,), (0,))).astype(BF)
-    d_hid = dot(dy, wd, ((1,), (1,))).astype(BF).astype(F32)
-    sig = jax.nn.sigmoid(gate)
-    d_up = (d_hid * (gate * sig)).astype(BF)
-    d_gate = (d_hid * up * (sig * (1 + gate * (1 - sig)))).astype(BF)
-    d_wg = dot(a, d_gate, ((0,), (0,))).astype(BF)
-    d_wu = dot(a, d_up, ((0,), (0,))).astype(BF)
-    da = None
-    if deeper:
-        da = dot(d_gate, wg, ((1,), (1,))).astype(BF) + dot(d_up, wu, ((1,), (1,))).astype(BF)
-    return d_wg, d_wu, d_wd, da
-
-
 class Flow:
     pass
 
 
 def sync_kernel(side, tiles, *refs):
-    (dwg, dwu, dwd, wg, wu, wd, mg, mu, md, vg, vu, vd,
+    (a1, a1t, a0, a0t, dy_in, h1, wg2, wu2, wd2, wg, wu, wd, mg, mu, md, vg, vu, vd,
      og, ou, od, omg, omu, omd, ovg, ovu, ovd,
-     L, R1, R2, MV, W, NW, D, R1d, R2d, MVd, Wd, NWd,
-     ss, rs, ssd, rsd, ls, lsd, ld, ldd) = refs
+     L, R1, R2, MV, W, NW, D, R1d, R2d, MVd, Wd, NWd, A, AT, DY, DA, HT, DGU, TW, TD,
+     ss, rs, ssd, rsd, ls, lsd, lt, la) = refs
+    tokens, d = A.shape
+    block = 512
     rep, me = lax.axis_index("rep"), lax.axis_index("dp")
     x, y = me // side, me % side
 
@@ -65,9 +47,12 @@
     def at(xx, yy):
         return (rep, mod(xx) * side + mod(yy))
 
+    for src, dst, sem in ((a1, A, la.at[0]), (a1t, AT, la.at[1]), (dy_in, DY, la.at[2])):
+        pltpu.make_async_copy(src, dst, sem).start()
     barrier = pltpu.get_barrier_semaphore()
     for dx, dy in ((1, 0), (-1, 0), (0, 1), (0, -1)):
         pl.semaphore_signal(barrier, inc=1, device_id=at(x + dx, y + dy), device_id_type=MESH)
+    DA[...] = jnp.zeros_like(DA)
     pl.semaphore_wait(barrier, 4)
 
     slots = tiles
@@ -103,7 +88,7 @@
     def down(ab):
         fl = Flow()
         lane = lambda c: pl.ds(128 * (4 * ab + c), 128)
-        fl.local = lambda c, t: D.at[t, :, :, :, lane(c)]
+        fl.local = lambda c, t: D.at[t, :, :, :, :, lane(c)]
         fl.r1 = lambda c, t, s: R1d.at[ab, c, s]
         fl.r2 = lambda c, t, s: R2d.at[ab, c, s]
         fl.nw = lambda c, t: NWd.at[ab, c]
@@ -111,11 +96,11 @@
         fl.mv = lambda c, t: (MVd.at[ab, c, 0], MVd.at[ab, c, 1])
         fl.w = lambda c, t: Wd.at[ab, c]
         fl.ls = lambda c, t, k: lsd.at[ab, c, k]
-        fl.out = lambda c, t: od.at[t, :, :, :, lane(c)]
+        fl.out = lambda c, t: od.at[t, :, :, :, :, lane(c)]
 
         def hbm(c, t):
-            cut = (t, slice(None), lane(c))
-            return md.at[cut], vd.at[cut], wd.at[t, x, y, :, lane(c)], omd.at[cut], ovd.at[cut]
+            cut = (t, slice(None), slice(None), lane(c))
+            return md.at[cut], vd.at[cut], wd.at[t, x, y, :, :, lane(c)], omd.at[cut], ovd.at[cut]
 
         fl.hbm = hbm
         return fl
@@ -193,12 +178,89 @@
         if k < 12:
             copy(k).start()
 
-    def load(c, t):
-        layer, j = tile_of(c, t)
-        return pltpu.make_async_copy((dwg, dwu)[c % 2].at[layer, :, :, :, pl.ds(j, TILE)], L.at[t % 3, c], ld.at[t % 2, c])
-
-    for layer in (0, 1):
-        pltpu.make_async_copy(dwd.at[layer], D.at[layer], ldd.at[layer]).start()
+    def tile_loads(g):
+        layer, j, par = 1 - g // tiles, pl.multiple_of((g % tiles) * TILE, TILE), g % 2
+        cols = pl.ds(j, TILE)
+        return (pltpu.make_async_copy(wg2.at[layer, :, cols], TW.at[par, :, :TILE], lt.at[par, 0]),
+                pltpu.make_async_copy(wu2.at[layer, :, cols], TW.at[par, :, TILE:], lt.at[par, 1]),
+                pltpu.make_async_copy(wd2.at[layer, cols, :], TD.at[par], lt.at[par, 2]))
+
+    def state_load(n):
+        src, dst = ((a1, A), (a1t, AT), (dy_in, DY), (h1, A), (a0, A), (a0t, AT))[n]
+        return pltpu.make_async_copy(src, dst, la.at[n])
+
+    def forth_and_back(g):
+        layer, par = 1 - g // tiles, g % 2
+
+        @pl.when(g + 1 < 2 * tiles)
+        def _():
+            for one in tile_loads(g + 1):
+                one.start()
+
+        for one in tile_loads(g):
+            one.wait()
+
+        def some(b, carry):
+            rows = pl.ds(pl.multiple_of(b * block, block), block)
+            both = dot(A[rows, :], TW[par], ((1,), (0,)))
+            gate, up = both[:, :TILE], both[:, TILE:]
+            d_hid = dot(DY[rows, :], TD[par], ((1,), (1,))).astype(BF).astype(F32)
+            sig = jax.nn.sigmoid(gate)
+            silu = gate * sig
+            HT[:, rows] = (silu * up).astype(BF).T
+            DGU[rows, TILE:] = (d_hid * silu).astype(BF)
+            DGU[rows, :TILE] = (d_hid * up * (sig * (1 + gate * (1 - sig)))).astype(BF)
+
+            @pl.when(layer == 1)
+            def _():
+                DA[rows, :] += dot(DGU[rows, :], TW[par], ((1,), (1,)))
+
+            return carry
+
+        lax.fori_loop(0, tokens // block, some, 0)
+
+    def gradients(g, slot, c):
+        layer, j = 1 - g // tiles, g % tiles
+        rows = TILE // 16
+
+        def of_gate_and_up(q, carry):
+            both = dot(AT[pl.ds(pl.multiple_of(q * 256, 256), 256), :], DGU[...], ((1,), (0,))).astype(BF)
+            L[slot % 3, c, q] = both[:, :TILE].reshape(side, -1, TILE)
+            L[slot % 3, c + 1, q] = both[:, TILE:].reshape(side, -1, TILE)
+            return carry
+
+        lax.fori_loop(0, side, of_gate_and_up, 0)
+
+        def of_down(n, carry):
+            lanes = pl.ds(pl.multiple_of(n * 256, 256), 256)
+            one = dot(HT[...], DY[:, lanes], ((1,), (0,))).astype(BF)
+            for i in range(rows):
+                r = j * rows + i
+                per = D.shape[3]
+                D[layer, r // (side * per), (r // per) % side, r % per, :, lanes] = one[16 * i : 16 * i + 16]
+            return carry
+
+        lax.fori_loop(0, d // 256, of_down, 0)
+
+    def to_the_first_layer():
+        state_load(3).start()
+        state_load(3).wait()
+
+        def some(b, carry):
+            rows = pl.ds(pl.multiple_of(b * 256, 256), 256)
+            h = A[rows, :].astype(F32)
+            scale = lax.rsqrt(jnp.mean(h * h, -1, keepdims=True) + 1e-6)
+            da = DA[rows, :].astype(BF).astype(F32)
+            inner = jnp.mean(h * da, -1, keepdims=True)
+            back = (scale * (da - h * (scale * scale * inner))).astype(BF)
+            DY[rows, :] = (DY[rows, :].astype(F32) + back.astype(F32)).astype(BF)
+            return carry
+
+        lax.fori_loop(0, tokens // 256, some, 0)
+        for n in (4, 5):
+            state_load(n).start()
+        for n in (4, 5):
+            state_load(n).wait()
 
     def round_(i, rho):
         for k in range(12, -1, -1):
@@ -210,8 +272,6 @@
                     @pl.when((t >= 0) & (t < slots))
                     def _():
                         for c in (2 * pair, 2 * pair + 1):
-                            if k == 0:
-                                load(c, t).wait()
                             stage(gu, c, t, k)
             for ab in (0, 1):
                 off = 2 * ab
@@ -222,35 +282,51 @@
                     @pl.when((i0 == a) | (i0 == b))
                     def _():
                         layer = jnp.where(i0 == a, 1, 0)
-                        if k == 0 and ab == 0:
-                            pltpu.make_async_copy(dwd.at[layer], D.at[layer], ldd.at[layer]).wait()
                         for c in range(4):
                             stage(downs[ab], c, layer, k)
 
     def turn(i, carry):
-        @pl.when(i < slots)
-        def _():
-            for c in range(4):
-                load(c, i).start()
-
-        for rho in range(4):
-            round_(i, rho)
+        for half in (0, 1):
+            g = 2 * i + half
+            round_(i, 2 * half)
+
+            if half:
+                @pl.when(g == tiles)
+                def _():
+                    to_the_first_layer()
+
+            @pl.when(i < slots)
+            def _():
+                forth_and_back(g)
+
+            round_(i, 2 * half + 1)
+
+            @pl.when(i < slots)
+            def _():
+                gradients(g, i, 2 * half)
+
         return carry
 
+    for one in tile_loads(0):
+        one.start()
+    for n in range(3):
+        state_load(n).wait()
     lax.fori_loop(0, slots + 4, turn, 0)
 
 
-def synced(mesh, d_ws, ws, ms, vs):
+def synced(mesh, states, ws, ms, vs):
     n = mesh.shape["dp"]
     side = math.isqrt(n)
     layers, d, ff = ws[0].shape
+    tokens = states[0].shape[0]
     tiles = ff // TILE
-    cut = lambda a: a.reshape(layers, side, side, a.shape[1] // n, a.shape[2])
-    rows, rowsd = d // n, ff // n
+    rows, per = d // n, ff // n // 16
+    gu, dn = (rows, TILE), (per, 16, 128)
+    mats = ((rows, ff), (rows, ff), (per, 16, d))
     hbm = pl.BlockSpec(memory_space=pl.ANY)
-    ws5 = [cut(w) for w in ws]
-    out_shape = [jax.ShapeDtypeStruct(w.shape, BF) for w in ws5] + [jax.ShapeDtypeStruct(m.shape, F32) for m in (*ms, *vs)]
-    gu, dn = (rows, TILE), (rowsd, 128)
+    ws5 = [w.reshape(layers, side, side, *mat) for w, mat in zip(ws, mats)]
+    mvs = [t.reshape(layers, *mat) for t, mat in zip((*ms, *vs), mats * 2)]
+    out_shape = [jax.ShapeDtypeStruct(w.shape, BF) for w in ws5] + [jax.ShapeDtypeStruct(t.shape, F32) for t in mvs]
     dma = pltpu.SemaphoreType.DMA
     scratch = [
         pltpu.VMEM((3, 4, side, side, *gu), BF),
@@ -259,25 +335,33 @@
         pltpu.VMEM((4, 2, *gu), F32),
         pltpu.VMEM((4, *gu), BF),
         pltpu.VMEM((2, 4, *gu), BF),
-        pltpu.VMEM((layers, side, side, rowsd, d), BF),
+        pltpu.VMEM((layers, side, side, per, 16, d), BF),
         pltpu.VMEM((2, 4, 3, side, *dn), BF),
         pltpu.VMEM((2, 4, 3, *dn), BF),
         pltpu.VMEM((2, 4, 2, *dn), F32),
         pltpu.VMEM((2, 4, *dn), BF),
         pltpu.VMEM((2, 4, *dn), BF),
+        pltpu.VMEM((tokens, d), BF),
+        pltpu.VMEM((d, tokens), BF),
+        pltpu.VMEM((tokens, d), BF),
+        pltpu.VMEM((tokens, d), F32),
+        pltpu.VMEM((TILE, tokens), BF),
+        pltpu.VMEM((tokens, 2 * TILE), BF),
+        pltpu.VMEM((2, d, 2 * TILE), BF),
+        pltpu.VMEM((2, TILE, d), BF),
         dma((2, 4, 12)), dma((2, 4, 12)), dma((2, 4, 12)), dma((2, 4, 12)),
-        dma((4, 6)), dma((2, 4, 6)), dma((2, 4)), dma((2,)),
+        dma((4, 6)), dma((2, 4, 6)), dma((2, 3)), dma((6,)),
     ]
     res = pl.pallas_call(
         functools.partial(sync_kernel, side, tiles),
         out_shape=out_shape,
-        in_specs=[hbm] * 12,
+        in_specs=[hbm] * 18,
         out_specs=[hbm] * 9,
         scratch_shapes=scratch,
-        compiler_params=pltpu.CompilerParams(collective_id=0, has_side_effects=True, vmem_limit_bytes=60 * 2**20),
+        compiler_params=pltpu.CompilerParams(collective_id=0, has_side_effects=True, vmem_limit_bytes=67043328),
         name="sync",
-    )(*(cut(g) for g in d_ws), *ws5, *ms, *vs)
-    return [r.reshape(w.shape) for r, w in zip(res[:3], ws)] + list(res[3:])
+    )(*states, *ws, *ws5, *mvs)
+    return [r.reshape(w.shape) for r, w in zip(res, (*ws, *ms, *vs))]
 
 
 def solution(mesh):
@@ -288,13 +372,8 @@
         hid0 = (jax.nn.silu(g0) * u0).astype(BF)
         h1 = x + dot(hid0, wd[0], ((1,), (0,))).astype(BF)
         a1, s1 = normed(h1)
-        g1, u1 = gate_up(a1, wg[1], wu[1])
-        hid1 = (jax.nn.silu(g1) * u1).astype(BF)
-        d_wg1, d_wu1, d_wd1, da = back(a1, g1, u1, hid1, dy, wg[1], wu[1], wd[1], True)
-        dh1 = dy + normed_back(h1, s1, da)
-        d_wg0, d_wu0, d_wd0, _ = back(a0, g0, u0, hid0, dh1, wg[0], wu[0], wd[0], False)
-        grads = [jnp.stack(p) for p in ((d_wg0, d_wg1), (d_wu0, d_wu1), (d_wd0, d_wd1))]
-        return tuple(synced(mesh, grads, (wg, wu, wd), mv[:3], mv[3:]))
+        states = (a1, a1.T, a0, a0.T, dy, h1)
+        return tuple(synced(mesh, states, (wg, wu, wd), mv[:3], mv[3:]))
 
     rd, rep, shard = P(("rep", "dp")), P(), P(None, "dp", None)
     out, outs = P("rep"), P("rep", "dp", None)

time: 808 us -> 581 us (0.72)
  matrix products: 317 us -> 57.3 us
  Pallas kernels: 410 us -> 471 us
  other arithmetic: 27.8 us -> 7.49 us
    dot_general x15 -> x3, matrix products: 317 us -> 57.3 us  [dot(): return lax.dot_general(a, b, (dims, ((), ())), preferred_element_type=F32)]
    pallas_call x1, Pallas kernels: 410 us -> 471 us  [synced(): pl.pallas_call(functools.partial(sync_kernel, side, tiles), out_shape=out...]
    another operation x2 -> x0, other arithmetic: 18.1 us -> none  [step(): jnp.stack(p)]
    unnamed x55 -> x33, local copies, waits for them, and re-layouts: 44.6 us -> 31.6 us
    transpose x0 -> x2, local copies, waits for them, and re-layouts: none -> 13 us  [step(): states = (a1, a1.T, a0, a0.T, dy, h1)]
where the time goes in v2:
time: 581 us
  Pallas kernels  471 us (81%)
  matrix products  57.3 us (10%)
  local copies, waits for them, and re-layouts  44.6 us (8%)
  other arithmetic  7.49 us (1%)
    pallas_call x1, Pallas kernels, synced(): pl.pallas_call(functools.partial(sync_kernel, side, tiles), out_shape=out...  471 us
    dot_general x3, matrix products, dot(): return lax.dot_general(a, b, (dims, ((), ())), preferred_element_type=F32)  57.3 us
    unnamed x33, local copies, waits for them, and re-layouts  31.6 us
    transpose x2, local copies, waits for them, and re-layouts, step(): states = (a1, a1.T, a0, a0.T, dy, h1)  13 us

profile of v2, /device:TPU:96, one launch (start us, length us, event | category | flops | bytes accessed | tf_op | source)
XLA Modules:
  0.0 580.6 jit_solution(1883181853479055369)
XLA Ops:
  0.6 3.1 fusion
  3.7 0.0 copy-start.1
  3.7 20.0 %fusion.8 = f32[2048,2816]{1,0:T(8,128)} fusion(bf16[2,1024,2816]{2,1,0:T(8,128)(2,1)} %refs_6_.1, bf16[1,2048,1024]{2,1,0:T(8,128)(2,1)} %param.11, f32[2048]{0:T(1024)S(1)} %add_rsqrt_fusion.1), kind=kOutput, calls=%fused_computation.13 | convolution fusion | flops 11817451520 | bytes 33038336 | tf_op jit(solution)/shard_map/dot_general | solution.py:17
  23.8 0.0 copy-done.1
  23.8 20.3 %multiply_convert_fusion.clone.3.clone.5 = bf16[2048,2816]{1,0:T(8,128)(2,1)} fusion(f32[2048,2816]{1,0:T(8,128)} %fusion.8, bf16[2,1024,2816]{2,1,0:T(8,128)(2,1)} %refs_7_.1, bf16[1,2048,1024]{2,1,0:T(8,128)(2,1)S(1)} %copy-done.1, f32[2048]{0:T(1024)S(1)} %add_rsqrt_fusion.1), kind=kOutput, calls=%fused_computation.clone.clone.clone.clone.clone.clone.clone.2 | convolution fusion | flops 11852054528 | bytes 44572672 | tf_op jit(solution)/shard_map/dot_general | solution.py:17
  44.1 16.9 %fusion.2 = (f32[2048]{0:T(1024)S(1)}, bf16[2048,1024]{1,0:T(8,128)(2,1)S(1)}) fusion(bf16[2,2816,1024]{2,1,0:T(8,128)(2,1)} %refs_8_.1, bf16[1,2048,1024]{2,1,0:T(8,128)(2,1)S(1)} %copy-done.1, bf16[2048,2816]{1,0:T(8,128)(2,1)} %multiply_convert_fusion.clone.3.clone.5), kind=kOutput, calls=%fused_computation.7 | convolution fusion | flops 11821643776 | bytes 25698304 | tf_op jit(solution)/shard_map/dot_general | solution.py:17
  61.0 0.0 copy-start
  61.0 4.4 fusion.1
  65.4 0.1 copy-done
  65.5 6.4 %copy.21.refs_1_ = bf16[1024,2048]{1,0:T(8,128)(2,1)} copy(bf16[1024,2048]{0,1:T(8,128)(2,1)} %bitcast.58) | data formatting | bytes 8388608 | tf_op jit(solution)/shard_map/transpose | solution.py:375
  72.0 6.5 %copy.22.refs_3_ = bf16[1024,2048]{1,0:T(8,128)(2,1)} copy(bf16[1024,2048]{0,1:T(8,128)(2,1)} %bitcast.57) | data formatting | bytes 8388608 | tf_op jit(solution)/shard_map/transpose | solution.py:375
  78.5 470.5 %sync.1 = (bf16[2,4,4,64,2816]{4,3,2,1,0:T(8,128)(2,1)}, bf16[2,4,4,64,2816]{4,3,2,1,0:T(8,128)(2,1)}, bf16[2,4,4,11,16,1024]{5,4,3,2,1,0:T(8,128)(2,1)}, f32[2,...) custom-call(bf16[2048,1024]{1,0:T(8,128)(2,1)} %get-tuple-element.30, ...), custom_call_target="tpu_custom_call" | custom-call | tf_op jit(solution)/shard_map/sync/pallas_call | solution.py:355
  549.0 0.0 copy-start.2
  549.0 0.0 slice-start
  549.0 0.0 slice-start.1
  549.0 11.7 %copy.33 = bf16[2,1024,2816]{2,1,0:T(8,128)(2,1)} copy(bf16[2,1024,2816]{2,1,0:T(8,128)(2,1)} %bitcast.63) | data formatting | bytes 23068672
  560.7 0.0 copy-done.2
  560.7 0.0 slice-start.2
  560.7 5.8 %copy.34 = bf16[2,1024,2816]{2,1,0:T(8,128)(2,1)} copy(bf16[2,1024,2816]{2,1,0:T(8,128)(2,1)S(1)} %bitcast.62) | data formatting | bytes 23068672
  566.6 0.0 slice-done
  566.6 0.7 slice-done.1
  567.3 1.3 slice-done.2
  568.6 0.0 copy-start.8
  568.6 0.0 copy-start.7
  568.6 0.0 copy-start.6
  568.6 5.4 copy.35
  574.0 0.0 copy-done.8
  574.0 0.0 copy-start.5
  574.0 0.0 copy-start.4
  574.0 0.0 copy-start.3
  574.0 1.1 copy.36
  575.1 0.0 copy-done.7
  575.1 1.1 copy.37
  576.2 0.0 copy-done.6
  576.2 1.1 copy.38
  577.3 0.0 copy-done.5
  577.3 1.1 copy.39
  578.4 0.0 copy-done.4
  578.4 1.1 copy.40
  579.5 0.0 copy-done.3
  579.5 1.1 copy.41
  (3 shorter events, 0.0 us)
Async XLA Ops:
  3.7 20.0 %copy-start.1 = (bf16[1,2048,1024]{2,1,0:T(8,128)(2,1)S(1)}, bf16[1,2048,1024]{2,1,0:T(8,128)(2,1)}, u32[]{:S(2)}) copy-start(bf16[1,2048,1024]{2,1,0:T(8,128)(2,1)} %param.11) | copy-start | bytes 12582916
  61.0 4.5 copy-start
  549.0 11.7 %copy-start.2 = (bf16[2,4,4,64,2816]{4,3,2,1,0:T(8,128)(2,1)S(1)}, bf16[2,4,4,64,2816]{4,3,2,1,0:T(8,128)(2,1)}, u32[]{:S(2)}) copy-start(bf16[2,4,4,64,2816]{4,3,2,1,0:T(8,128)(2,1)} %get-tuple-element.19) | copy-start | bytes 34603012
  549.0 17.6 %slice-start = ((s8[11534336]{0:T(1024)(128)(4,1)}), s8[4194304]{0:T(1024)(128)(4,1)S(1)}, s32[]{:S(2)}) async-start(s8[11534336]{0:T(1024)(128)(4,1)} %bitcast.59), calls=%async_computation | async-start | bytes 8388608
  549.0 18.2 %slice-start.1 = ((s8[11534336]{0:T(1024)(128)(4,1)}), s8[4194304]{0:T(1024)(128)(4,1)S(1)}, s32[]{:S(2)}) async-start(s8[11534336]{0:T(1024)(128)(4,1)} %bitcast.59), calls=%async_computation.1 | async-start | bytes 8388608
  560.7 7.8 %slice-start.2 = ((s8[11534336]{0:T(1024)(128)(4,1)}), s8[3145728]{0:T(1024)(128)(4,1)S(1)}, s32[]{:S(2)}) async-start(s8[11534336]{0:T(1024)(128)(4,1)} %bitcast.59), calls=%async_computation.2 | async-start | bytes 6291456
  568.6 5.4 copy-start.8
  568.6 6.5 %copy-start.7 = (f32[2,64,2816]{2,1,0:T(8,128)S(1)}, f32[2,64,2816]{2,1,0:T(8,128)}, u32[]{:S(2)}) copy-start(f32[2,64,2816]{2,1,0:T(8,128)} %get-tuple-element.44) | copy-start | bytes 4325380
  568.6 7.6 %copy-start.6 = (f32[2,11,16,1024]{3,2,1,0:T(8,128)S(1)}, f32[2,11,16,1024]{3,2,1,0:T(8,128)}, u32[]{:S(2)}) copy-start(f32[2,11,16,1024]{3,2,1,0:T(8,128)} %get-tuple-element.23) | copy-start | bytes 4325380
  574.0 3.3 copy-start.5
  574.0 4.4 copy-start.4
  574.0 5.5 copy-start.3

commit v3 on v2

v3 whole, which is shorter than its diff:
```python
import functools
import math

import jax
import jax.numpy as jnp
from jax import lax
from jax.experimental import pallas as pl
from jax.experimental.pallas import tpu as pltpu
from jax.sharding import PartitionSpec as P

BF, F32 = jnp.bfloat16, jnp.float32
MESH = pl.DeviceIdType.MESH
TILE = 256


def dot(a, b, dims):
    return lax.dot_general(a, b, (dims, ((), ())), preferred_element_type=F32)


class Flow:
    pass


def sync_kernel(side, tiles, *refs):
    (a1, a1t, a0, a0t, dy_in, h1, h0t, wg2, wu2, wd2, wg, wu, wd, mg, mu, md, vg, vu, vd,
     og, ou, od, omg, omu, omd, ovg, ovu, ovd, kept,
     L, R1, R1c, R2, MV, W, NW, D, R1d, R2d, MVd, Wd, NWd, A, AT, DY, DA, HT, DGU, TW, TD,
     ss, rs, ssd, rsd, ls, lsd, lt, la, lk, lh) = refs
    tokens, d = A.shape
    block = 1024
    rep, me = lax.axis_index("rep"), lax.axis_index("dp")
    x, y = lax.div(me, side), lax.rem(me, side)
    xs, ys = ([lax.rem(v + n, side) for n in range(side)] for v in (x, y))

    def at(dx, dy):
        return (rep, xs[dx % side] * side + ys[dy % side])

    for src, dst, n in ((a1, A, 0), (dy_in, DY, 1), (a1t, AT, 2)):
        pltpu.make_async_copy(src, dst, la.at[n]).start()
    barrier = pltpu.get_barrier_semaphore()
    for dx, dy in ((1, 0), (-1, 0), (0, 1), (0, -1)):
        pl.semaphore_signal(barrier, inc=1, device_id=at(dx, dy), device_id_type=MESH)
    DA[...] = jnp.zeros_like(DA)
    pl.semaphore_wait(barrier, 4)

    def tile_of(c, t):
        g = 2 * t + c // 2
        past = g >= tiles
        return jnp.where(past, 0, 1), pl.multiple_of((g - jnp.where(past, tiles, 0)) * TILE, TILE)

    gu = Flow()
    gu.local = lambda c, t: L.at[lax.rem(t, 3), c]
    gu.r1 = lambda c, t, s: R1c.at[lax.rem(t, 3), c] if s == 2 else R1.at[lax.rem(t, 2), c, s]
    gu.r2 = lambda c, t, s: R2.at[lax.rem(t, 2), c, s]
    gu.nw = lambda c, t: NW.at[lax.rem(t, 2), c]
    gu.sems = lambda c, t, k: (ss.at[lax.rem(t, 2), c, k], rs.at[lax.rem(t, 2), c, k])
    gu.mv = lambda c, t: (MV.at[c, 0], MV.at[c, 1])
    gu.w = lambda c, t: W.at[c]
    gu.ls = lambda c, t, k: ls.at[c, k]

    def gu_out(c, t):
        layer, j = tile_of(c, t)
        return (og, ou)[c % 2].at[layer, :, :, :, pl.ds(j, TILE)]

    def gu_hbm(c, t):
        layer, j = tile_of(c, t)
        kind = c % 2
        cut = (layer, slice(None), pl.ds(j, TILE))
        return ((mg, mu)[kind].at[cut], (vg, vu)[kind].at[cut], (wg, wu)[kind].at[layer, x, y, :, pl.ds(j, TILE)],
                (omg, omu)[kind].at[cut], (ovg, ovu)[kind].at[cut])

    gu.out, gu.hbm = gu_out, gu_hbm

    def down(ab):
        fl = Flow()
        lane = lambda c: pl.ds(128 * (4 * ab + c), 128)
        fl.local = lambda c, t: D.at[t, :, :, :, :, lane(c)]
        fl.r1 = lambda c, t, s: R1d.at[ab, c, s]
        fl.r2 = lambda c, t, s: R2d.at[ab, c, s]
        fl.nw = lambda c, t: NWd.at[ab, c]
        fl.sems = lambda c, t, k: (ssd.at[ab, c, k], rsd.at[ab, c, k])
        fl.mv = lambda c, t: (MVd.at[ab, c, 0], MVd.at[ab, c, 1])
        fl.w = lambda c, t: Wd.at[ab, c]
        fl.ls = lambda c, t, k: lsd.at[ab, c, k]
        fl.out = lambda c, t: od.at[t, :, :, :, :, lane(c)]

        def hbm(c, t):
            cut = (t, slice(None), slice(None), lane(c))
            return md.at[cut], vd.at[cut], wd.at[t, x, y, :, :, lane(c)], omd.at[cut], ovd.at[cut]

        fl.hbm = hbm
        return fl

    downs = (down(0), down(1))

    toward = {(axis, sg): at(*((sg, 0) if axis == 0 else (0, sg))) for axis in (0, 1) for sg in (1, -1)}

    def stage(fl, c, t, k):
        first, sg = c < 2, (1, -1)[c % 2]
        r1, r2 = (xs, ys) if first else (ys, xs)
        p1, p2 = r1[0], r2[0]
        nb1, nb2 = (toward[0, sg], toward[1, sg]) if first else (toward[1, sg], toward[0, sg])
        loc = fl.local(c, t)

        def turned(r, n):
            return r[(-sg * n) % side]

        def chunk(ref, q):
            return ref.at[q] if first else ref.at[:, q]

        def sub(ref, q, q2):
            return ref.at[q, q2] if first else ref.at[q2, q]

        def copy(k):
            send, recv = fl.sems(c, t, k)
            if k < 3:
                src, dst, to = chunk(loc, turned(r1, 1 + k)), fl.r1(c, t, k), nb1
            elif k < 6:
                src, dst, to = sub(loc, p1, turned(r2, k - 2)), fl.r2(c, t, k - 3), nb2
            elif k < 9:
                dst, to = sub(fl.out(c, t), p1, turned(r2, k - 6)), nb2
                src = fl.nw(c, t) if k == 6 else dst
            else:
                dst, to = chunk(fl.out(c, t), turned(r1, k - 9)), nb1
                src = dst
            return pltpu.make_async_remote_copy(src, dst, send, recv, device_id=to, device_id_type=MESH)

        def locals_(ins_too):
            hm, hv, hw, hom, hov = fl.hbm(c, t)
            bm, bv = fl.mv(c, t)
            own = sub(fl.out(c, t), p1, p2)
            s = lambda n: fl.ls(c, t, n)
            if ins_too:
                return [pltpu.make_async_copy(a, b, s(n)) for n, (a, b) in enumerate(((hm, bm), (hv, bv), (hw, fl.w(c, t))))]
            return [pltpu.make_async_copy(a, b, s(3 + n)) for n, (a, b) in enumerate(((bm, hom), (bv, hov), (fl.nw(c, t), own)))]

        if k > 0:
            copy(k - 1).wait()
        if k in (1, 2):
            mine = chunk(loc, turned(r1, 1 + k))
            mine[...] = (mine[...].astype(F32) + fl.r1(c, t, k - 1)[...].astype(F32)).astype(BF)
        elif k in (3, 4, 5):
            q2 = turned(r2, k - 2)
            mine = sub(loc, p1, q2)
            total = mine[...].astype(F32) + fl.r1(c, t, 2).at[q2][...].astype(F32)
            if k > 3:
                total += fl.r2(c, t, k - 4)[...].astype(F32)
            mine[...] = total.astype(BF)
            if k == 4:
                for one in locals_(True):
                    one.start()
        elif k == 6:
            total = sub(loc, p1, p2)[...].astype(F32) + fl.r1(c, t, 2).at[p2][...].astype(F32)
            g = (total + fl.r2(c, t, 2)[...].astype(F32)).astype(BF).astype(F32)
            for one in locals_(True):
                one.wait()
            bm, bv = fl.mv(c, t)
            m = 0.9 * bm[...] + 0.1 * g
            v = 0.95 * bv[...] + 0.05 * g * g
            w = fl.w(c, t)[...].astype(F32)
            bm[...] = m
            bv[...] = v
            fl.nw(c, t)[...] = (w - 0.02 * (m * lax.rsqrt(v + 1e-8) + 0.1 * w)).astype(BF)
            for one in locals_(False):
                one.start()
        elif k == 7:
            for one in locals_(False):
                one.wait()
        if k < 12:
            copy(k).start()

    middle = 2 * ((2 * tiles + 2 + 5) // 6)
    last = 2 * tiles + middle

    def tile_loads(layer, j, par, down=True):
        cols = pl.ds(pl.multiple_of(j * TILE, TILE), TILE)
        loads = [pltpu.make_async_copy(wg2.at[layer, :, cols], TW.at[par, :, :TILE], lt.at[par, 0]),
                 pltpu.make_async_copy(wu2.at[layer, :, cols], TW.at[par, :, TILE:], lt.at[par, 1])]
        return loads + ([pltpu.make_async_copy(wd2.at[layer, cols, :], TD.at[par], lt.at[par, 2])] if down else [])

    def state_load(n):
        src, dst = ((a1, A), (dy_in, DY), (a1t, AT), (h1, A), (a0, A), (a0t, AT))[n]
        return pltpu.make_async_copy(src, dst, la.at[n])

    def keep(j, par):
        return pltpu.make_async_copy(DGU.at[par], kept.at[j], lk.at[par])

    def take(j, par):
        return pltpu.make_async_copy(kept.at[j], DGU.at[par], lk.at[par])

    def hidden_load(j):
        rows = pl.ds(pl.multiple_of(j * TILE, TILE), TILE)
        return pltpu.make_async_copy(h0t.at[rows, :], HT.at[lax.rem(j, 2)], lh.at[lax.rem(j, 2)])

    def forth_and_back(layer, j, par):
        def some(b, carry):
            rows = pl.ds(pl.multiple_of(b * block, block), block)
            both = dot(A[rows, :], TW[par], ((1,), (0,)))
            gate, up = both[:, :TILE], both[:, TILE:]
            d_hid = dot(DY[rows, :], TD[par], ((1,), (1,))).astype(BF).astype(F32)
            sig = jax.nn.sigmoid(gate)
            silu = gate * sig
            if layer == 1:
                HT[par, :, rows] = (silu * up).astype(BF).T
            DGU[par, rows, TILE:] = (d_hid * silu).astype(BF)
            DGU[par, rows, :TILE] = (d_hid * up * (sig * (1 + gate * (1 - sig)))).astype(BF)
            return carry

        lax.fori_loop(0, tokens // block, some, 0)

    def of_gate_and_up(g, par):
        slot, c = lax.div(g, 2), 2 * lax.rem(g, 2)
        both = dot(AT[...], DGU[par], ((1,), (0,))).astype(BF)
        L[lax.rem(slot, 3), c] = both[:, :TILE].reshape(side, side, -1, TILE)
        L[lax.rem(slot, 3), c + 1] = both[:, TILE:].reshape(side, side, -1, TILE)

    def of_down(layer, j, par):
        one = dot(HT[par], DY[...], ((1,), (0,))).astype(BF)
        per = D.shape[3]
        for i in range(TILE // 16):
            r = j * (TILE // 16) + i
            D[layer, lax.div(r, side * per), lax.rem(lax.div(r, per), side), lax.rem(r, per)] = one[16 * i : 16 * i + 16]

    def of_input(par):
        def some(b, carry):
            rows = pl.ds(pl.multiple_of(b * block, block), block)
            DA[rows, :] += dot(DGU[par, rows, :], TW[par], ((1,), (1,)))
            return carry

        lax.fori_loop(0, tokens // block, some, 0)

    def norm_back():
        def some(b, carry):
            rows = pl.ds(pl.multiple_of(b * 256, 256), 256)
            h = A[rows, :].astype(F32)
            scale = lax.rsqrt(jnp.mean(h * h, -1, keepdims=True) + 1e-6)
            da = DA[rows, :].astype(BF).astype(F32)
            inner = jnp.mean(h * da, -1, keepdims=True)
            back = (scale * (da - h * (scale * scale * inner))).astype(BF)
            DY[rows, :] = (DY[rows, :].astype(F32) + back.astype(F32)).astype(BF)
            return carry

        lax.fori_loop(0, tokens // 256, some, 0)

    def compute(q):
        turn, part = lax.div(q, 3), lax.rem(q, 3)
        first, second = turn < tiles, (turn >= tiles + middle) & (turn < last)
        g = jnp.where(first, turn, turn - middle)
        j, par = g - jnp.where(first, 0, tiles), lax.rem(g, 2)

        @pl.when((part == 0) & first)
        def _():
            @pl.when(g + 1 < tiles)
            def _():
                for one in tile_loads(1, j + 1, 1 - par):
                    one.start()

            for one in tile_loads(1, j, par):
                one.wait()

            @pl.when(g >= 2)
            def _():
                keep(j - 2, par).wait()

            forth_and_back(1, j, par)

            @pl.when(j < tiles - 1)
            def _():
                keep(j, par).start()

        @pl.when((part == 0) & second)
        def _():
            @pl.when(g + 1 < 2 * tiles)
            def _():
                for one in tile_loads(0, j + 1, 1 - par):
                    one.start()

            for one in tile_loads(0, j, par):
                one.wait()
            forth_and_back(0, j, par)

        @pl.when((part == 1) & (first | second))
        def _():
            of_gate_and_up(g, par)

        p = q - 3 * tiles
        h = p - tiles - 1

        @pl.when(((part == 2) & first) | ((h >= 0) & (h < tiles)))
        def _():
            @pl.when(~first)
            def _():
                @pl.when(h + 1 < tiles)
                def _():
                    hidden_load(h + 1).start()

                hidden_load(h).wait()

            of_down(jnp.where(first, 1, 0), jnp.where(first, j, h), jnp.where(first, par, lax.rem(h, 2)))

        @pl.when((p >= 0) & (p < tiles))
        def _():
            @pl.when(p == 0)
            def _():
                keep(tiles - 2, 1).wait()
                state_load(3).start()
                state_load(5).start()

            @pl.when(p > 0)
            def _():
                take(p - 1, lax.rem(p, 2)).wait()
                for one in tile_loads(1, p - 1, lax.rem(p, 2), False):
                    one.wait()

            @pl.when(p + 1 < tiles)
            def _():
                take(p, 1 - lax.rem(p, 2)).start()
                for one in tile_loads(1, p, 1 - lax.rem(p, 2), False):
                    one.start()

            of_input(lax.rem(p, 2))

        @pl.when(p == tiles)
        def _():
            hidden_load(0).start()
            for one in tile_loads(0, 0, tiles % 2):
                one.start()
            state_load(3).wait()
            norm_back()
            state_load(4).start()

        @pl.when(q == 3 * (tiles + middle) - 1)
        def _():
            state_load(4).wait()
            state_load(5).wait()

    def subround(q):
        six = lax.div(q, 6)
        place = q - 6 * six
        for z in range(6):

            @pl.when(place == z)
            def _():
                for k in range(12, -1, -1):
                    if (z - 2 - 2 * k) % 3 == 0:
                        turn = 2 * six + (z - 2 - 2 * k) // 3
                        second = turn >= tiles + middle
                        g = turn - jnp.where(second, middle, 0)

                        @pl.when(((turn >= 0) & (turn < tiles)) | (second & (turn < last)))
                        def _():
                            for c in (2 * (z % 2), 2 * (z % 2) + 1):
                                stage(gu, c, lax.div(g, 2), k)

        for ab in (0, 1):

            @pl.when((q >= 3 * tiles) & (lax.rem(q, 2) == (tiles + ab) % 2))
            def _():
                for k in range(12, -1, -1):
                    at1, at0 = 3 * tiles + ab + 2 * k, 3 * (tiles + middle) + ab + 2 * k

                    @pl.when((q == at1) | (q == at0))
                    def _():
                        for c in range(4):
                            stage(downs[ab], c, jnp.where(q == at1, 1, 0), k)

    def body(q, carry):
        compute(q)
        subround(q)
        return carry

    for one in tile_loads(1, 0, 0):
        one.start()
    for n in range(3):
        state_load(n).wait()
    lax.fori_loop(0, 3 * last + 2 + 2 * 12, body, 0)


def first_kernel(tiles, x_in, wg2, wu2, wd2, h1, a1, a1t, a0, a0t, h0t, X, A, AT, ACC, HN, HT, TW, TD, lt, lx, lh, lo):
    tokens, d = X.shape
    block, part = 1024, 512

    def tile_loads(j):
        par = lax.rem(j, 2)
        cols = pl.ds(pl.multiple_of(j * TILE, TILE), TILE)
        return (pltpu.make_async_copy(wg2.at[0, :, cols], TW.at[par, :, :TILE], lt.at[par, 0]),
                pltpu.make_async_copy(wu2.at[0, :, cols], TW.at[par, :, TILE:], lt.at[par, 1]),
                pltpu.make_async_copy(wd2.at[0, cols, :], TD.at[lax.rem(j, 3)], lt.at[par, 2]))

    def x_load(n):
        rows = pl.ds(pl.multiple_of(n * part, part), part)
        return pltpu.make_async_copy(x_in.at[rows, :], X.at[rows, :], lx.at[n])

    def hidden_out(j):
        return pltpu.make_async_copy(HT.at[j % 2], h0t.at[pl.ds(pl.multiple_of(j * TILE, TILE), TILE), :], lh.at[j % 2])

    def norm(rows, h):
        a = (h * lax.rsqrt(jnp.mean(h * h, -1, keepdims=True) + 1e-6)).astype(BF)
        A[rows, :] = a
        AT[:, rows] = a.T

    for n in range(tokens // part):
        x_load(n).start()
    for one in tile_loads(0):
        one.start()
    ACC[...] = jnp.zeros_like(ACC)
    HN[1] = jnp.zeros((tokens, TILE), BF)
    TD[2] = jnp.zeros((TILE, d), BF)

    def begin(n, carry):
        x_load(n).wait()
        rows = pl.ds(pl.multiple_of(n * part, part), part)
        norm(rows, X[rows, :].astype(F32))
        return carry

    lax.fori_loop(0, tokens // part, begin, 0)
    outs = [pltpu.make_async_copy(A, a0, lo.at[0]), pltpu.make_async_copy(AT, a0t, lo.at[1])]
    for one in outs:
        one.start()

    def turn(j, carry):
        par = j % 2

        @pl.when(j + 1 < tiles)
        def _():
            for one in tile_loads(j + 1):
                one.start()

        for one in tile_loads(j):
            one.wait()

        @pl.when(j >= 2)
        def _():
            hidden_out(j - 2).wait()

        def some(b, carry):
            rows = pl.ds(pl.multiple_of(b * block, block), block)
            both = dot(A[rows, :], TW[par], ((1,), (0,)))
            ACC[rows, :] += dot(HN[1 - par, rows, :], TD[lax.rem(j + 2, 3)], ((1,), (0,)))
            gate, up = both[:, :TILE], both[:, TILE:]
            hid = (gate * jax.nn.sigmoid(gate) * up).astype(BF)
            HN[par, rows, :] = hid
            HT[par, :, rows] = hid.T
            return carry

        lax.fori_loop(0, tokens // block, some, 0)
        hidden_out(j).start()
        return carry

    lax.fori_loop(0, tiles, turn, 0)

    def last_down(b, carry):
        rows = pl.ds(pl.multiple_of(b * block, block), block)
        ACC[rows, :] += dot(HN[(tiles - 1) % 2, rows, :], TD[(tiles - 1) % 3], ((1,), (0,)))
        return carry

    lax.fori_loop(0, tokens // block, last_down, 0)
    for one in outs:
        one.wait()
    hidden_out(tiles - 2).wait()
    hidden_out(tiles - 1).wait()

    def end(n, carry):
        rows = pl.ds(pl.multiple_of(n * part, part), part)
        h = (X[rows, :].astype(F32) + ACC[rows, :].astype(BF).astype(F32)).astype(BF)
        X[rows, :] = h
        norm(rows, h.astype(F32))
        return carry

    lax.fori_loop(0, tokens // part, end, 0)
    outs = [pltpu.make_async_copy(A, a1, lo.at[0]), pltpu.make_async_copy(AT, a1t, lo.at[1]), pltpu.make_async_copy(X, h1, lo.at[2])]
    for one in outs:
        one.start()
    for one in outs:
        one.wait()


def first(x, wg, wu, wd):
    tokens, d = x.shape
    ff = wg.shape[2]
    tiles = ff // TILE
    hbm = pl.BlockSpec(memory_space=pl.ANY)
    dma = pltpu.SemaphoreType.DMA
    wide, tall, hid = (jax.ShapeDtypeStruct(t, BF) for t in ((tokens, d), (d, tokens), (ff, tokens)))
    return pl.pallas_call(
        functools.partial(first_kernel, tiles),
        out_shape=[wide, wide, tall, wide, tall, hid],
        in_specs=[hbm] * 4,
        out_specs=[hbm] * 6,
        scratch_shapes=[
            pltpu.VMEM((tokens, d), BF), pltpu.VMEM((tokens, d), BF), pltpu.VMEM((d, tokens), BF), pltpu.VMEM((tokens, d), F32),
            pltpu.VMEM((2, tokens, TILE), BF), pltpu.VMEM((2, TILE, tokens), BF),
            pltpu.VMEM((2, d, 2 * TILE), BF), pltpu.VMEM((3, TILE, d), BF),
            dma((2, 3)), dma((4,)), dma((2,)), dma((3,)),
        ],
        compiler_params=pltpu.CompilerParams(vmem_limit_bytes=60 * 2**20),
        name="first",
    )(x, wg, wu, wd)


def synced(mesh, states, ws, ms, vs):
    n = mesh.shape["dp"]
    side = math.isqrt(n)
    layers, d, ff = ws[0].shape
    tokens = states[0].shape[0]
    tiles = ff // TILE
    rows, per = d // n, ff // n // 16
    gu, dn = (rows, TILE), (per, 16, 128)
    mats = ((rows, ff), (rows, ff), (per, 16, d))
    hbm = pl.BlockSpec(memory_space=pl.ANY)
    ws5 = [w.reshape(layers, side, side, *mat) for w, mat in zip(ws, mats)]
    mvs = [t.reshape(layers, *mat) for t, mat in zip((*ms, *vs), mats * 2)]
    out_shape = [jax.ShapeDtypeStruct(w.shape, BF) for w in ws5] + [jax.ShapeDtypeStruct(t.shape, F32) for t in mvs]
    out_shape.append(jax.ShapeDtypeStruct((tiles, tokens, 2 * TILE), BF))
    dma = pltpu.SemaphoreType.DMA
    scratch = [
        pltpu.VMEM((3, 4, side, side, *gu), BF),
        pltpu.VMEM((2, 4, 2, side, *gu), BF),
        pltpu.VMEM((3, 4, side, *gu), BF),
        pltpu.VMEM((2, 4, 3, *gu), BF),
        pltpu.VMEM((4, 2, *gu), F32),
        pltpu.VMEM((4, *gu), BF),
        pltpu.VMEM((2, 4, *gu), BF),
        pltpu.VMEM((layers, side, side, per, 16, d), BF),
        pltpu.VMEM((2, 4, 3, side, *dn), BF),
        pltpu.VMEM((2, 4, 3, *dn), BF),
        pltpu.VMEM((2, 4, 2, *dn), F32),
        pltpu.VMEM((2, 4, *dn), BF),
        pltpu.VMEM((2, 4, *dn), BF),
        pltpu.VMEM((tokens, d), BF),
        pltpu.VMEM((d, tokens), BF),
        pltpu.VMEM((tokens, d), BF),
        pltpu.VMEM((tokens, d), F32),
        pltpu.VMEM((2, TILE, tokens), BF),
        pltpu.VMEM((2, tokens, 2 * TILE), BF),
        pltpu.VMEM((2, d, 2 * TILE), BF),
        pltpu.VMEM((2, TILE, d), BF),
        dma((2, 4, 12)), dma((2, 4, 12)), dma((2, 4, 12)), dma((2, 4, 12)),
        dma((4, 6)), dma((2, 4, 6)), dma((2, 3)), dma((6,)), dma((2,)), dma((2,)),
    ]
    res = pl.pallas_call(
        functools.partial(sync_kernel, side, tiles),
        out_shape=out_shape,
        in_specs=[hbm] * 19,
        out_specs=[hbm] * 10,
        scratch_shapes=scratch,
        compiler_params=pltpu.CompilerParams(collective_id=0, has_side_effects=True, vmem_limit_bytes=67043328),
        name="sync",
    )(*states, *ws, *ws5, *mvs)
    return [r.reshape(w.shape) for r, w in zip(res[:9], (*ws, *ms, *vs))]


def solution(mesh):
    def step(x, dy, wg, wu, wd, *mv):
        x, dy = x[0], dy[0]
        h1, a1, a1t, a0, a0t, h0t = first(x, wg, wu, wd)
        states = (a1, a1t, a0, a0t, dy, h1, h0t)
        return tuple(synced(mesh, states, (wg, wu, wd), mv[:3], mv[3:]))

    rd, rep, shard = P(("rep", "dp")), P(), P(None, "dp", None)
    out, outs = P("rep"), P("rep", "dp", None)
    return jax.shard_map(
        step,
        mesh=mesh,
        in_specs=(rd, rd, rep, rep, rep, *[shard] * 6),
        out_specs=(out, out, out, *[outs] * 6),
        check_vma=False,
    )
```

time: 581 us -> 515 us (0.89)
  matrix products: 57.3 us -> 0 us
  local copies, waits for them, and re-layouts: 44.6 us -> 31 us
  Pallas kernels: 471 us -> 483 us
  other arithmetic: 7.49 us -> 0.01 us
    dot_general x3 -> x0, matrix products: 57.3 us -> none  [dot(): return lax.dot_general(a, b, (dims, ((), ())), preferred_element_type=F32)]
    pallas_call x0 -> x1, Pallas kernels: none -> 53.7 us  [first(): pl.pallas_call(functools.partial(first_kernel, tiles), out_shape=[wide, w...]
    pallas_call x1, Pallas kernels: 471 us -> 430 us  [synced(): pl.pallas_call(functools.partial(sync_kernel, side, tiles), out_shape=out...]
    transpose x2 -> x0, local copies, waits for them, and re-layouts: 13 us -> none  [step(): states = (a1, a1.T, a0, a0.T, dy, h1)]
    unnamed x33 -> x29, local copies, waits for them, and re-layouts: 31.6 us -> 31 us
where the time goes in v3:
time: 515 us
  Pallas kernels  483 us (94%)
  local copies, waits for them, and re-layouts  31 us (6%)
    pallas_call x1, Pallas kernels, synced(): pl.pallas_call(functools.partial(sync_kernel, side, tiles), out_shape=out...  430 us
    pallas_call x1, Pallas kernels, first(): pl.pallas_call(functools.partial(first_kernel, tiles), out_shape=[wide, w...  53.7 us
    unnamed x29, local copies, waits for them, and re-layouts  31 us

profile of v3, /device:TPU:96, one launch (start us, length us, event | category | flops | bytes accessed | tf_op | source)
XLA Modules:
  0.0 515.1 jit_solution(9756652236705227717)
XLA Ops:
  0.6 53.7 %first.1 = (bf16[2048,1024]{1,0:T(8,128)(2,1)}, bf16[2048,1024]{1,0:T(8,128)(2,1)}, bf16[1024,2048]{1,0:T(8,128)(2,1)}, bf16[2048,1024]{1,0:T(8,128)(2,1)}, bf16...) custom-call(bf16[2048,1024]{1,0:T(8,128)(2,1)} %bitcast.21, bf16[2,1024,2816]{2,1,0:T(8,128)(2,1)} %refs_7_.1, ...), custom_call_target="tpu_custom_call" | custom-call | tf_op jit(solution)/shard_map/first/pallas_call | solution.py:485
  54.4 429.7 %sync.1 = (bf16[2,4,4,64,2816]{4,3,2,1,0:T(8,128)(2,1)}, bf16[2,4,4,64,2816]{4,3,2,1,0:T(8,128)(2,1)}, bf16[2,4,4,11,16,1024]{5,4,3,2,1,0:T(8,128)(2,1)}, f32[2,...) custom-call(bf16[2048,1024]{1,0:T(8,128)(2,1)} %get-tuple-element.24, ...), custom_call_target="tpu_custom_call" | custom-call | tf_op jit(solution)/shard_map/sync/pallas_call | solution.py:541
  484.1 0.0 copy-start
  484.1 0.0 slice-start
  484.1 0.0 slice-start.1
  484.1 11.7 %copy.29 = bf16[2,1024,2816]{2,1,0:T(8,128)(2,1)} copy(bf16[2,1024,2816]{2,1,0:T(8,128)(2,1)} %bitcast.19) | data formatting | bytes 23068672
  495.8 0.0 copy-done
  495.8 0.0 slice-start.2
  495.8 5.8 %copy.30 = bf16[2,1024,2816]{2,1,0:T(8,128)(2,1)} copy(bf16[2,1024,2816]{2,1,0:T(8,128)(2,1)S(1)} %bitcast.18) | data formatting | bytes 23068672
  501.6 0.0 slice-done
  501.6 0.7 slice-done.1
  502.3 1.3 slice-done.2
  503.6 0.0 copy-start.6
  503.6 0.0 copy-start.5
  503.6 4.8 copy.31
  508.5 0.0 copy-done.6
  508.5 0.0 copy-start.4
  508.5 0.0 copy-start.3
  508.5 1.1 copy.32
  509.6 0.0 copy-done.5
  509.6 0.0 copy-start.2
  509.6 1.1 copy.33
  510.7 0.0 copy-done.4
  510.7 0.0 copy-start.1
  510.7 1.1 copy.34
  511.8 0.0 copy-done.3
  511.8 1.1 copy.35
  512.9 0.0 copy-done.2
  512.9 1.1 copy.36
  514.0 0.0 copy-done.1
  514.0 1.1 copy.37
  (1 shorter events, 0.0 us)
Async XLA Ops:
  484.1 11.7 %copy-start = (bf16[2,4,4,64,2816]{4,3,2,1,0:T(8,128)(2,1)S(1)}, bf16[2,4,4,64,2816]{4,3,2,1,0:T(8,128)(2,1)}, u32[]{:S(2)}) copy-start(bf16[2,4,4,64,2816]{4,3,2,1,0:T(8,128)(2,1)} %get-tuple-element.31) | copy-start | bytes 34603012
  484.1 17.6 %slice-start = ((s8[11534336]{0:T(1024)(128)(4,1)}), s8[4194304]{0:T(1024)(128)(4,1)S(1)}, s32[]{:S(2)}) async-start(s8[11534336]{0:T(1024)(128)(4,1)} %bitcast.15), calls=%async_computation | async-start | bytes 8388608
  484.1 18.2 %slice-start.1 = ((s8[11534336]{0:T(1024)(128)(4,1)}), s8[4194304]{0:T(1024)(128)(4,1)S(1)}, s32[]{:S(2)}) async-start(s8[11534336]{0:T(1024)(128)(4,1)} %bitcast.15), calls=%async_computation.1 | async-start | bytes 8388608
  495.8 7.8 %slice-start.2 = ((s8[11534336]{0:T(1024)(128)(4,1)}), s8[3145728]{0:T(1024)(128)(4,1)S(1)}, s32[]{:S(2)}) async-start(s8[11534336]{0:T(1024)(128)(4,1)} %bitcast.15), calls=%async_computation.2 | async-start | bytes 6291456
  503.6 4.9 copy-start.6
  503.6 6.0 %copy-start.5 = (f32[2,64,2816]{2,1,0:T(8,128)S(1)}, f32[2,64,2816]{2,1,0:T(8,128)}, u32[]{:S(2)}) copy-start(f32[2,64,2816]{2,1,0:T(8,128)} %get-tuple-element.52) | copy-start | bytes 4325380
  508.5 2.2 copy-start.4
  508.5 3.3 copy-start.3
  509.6 3.3 copy-start.2
  510.7 3.3 copy-start.1

commit v4 on v3

--- a/solution.py
+++ b/solution.py
@@ -22,10 +22,10 @@
 
 
 def sync_kernel(side, tiles, *refs):
-    (a1, a1t, a0, a0t, dy_in, h1, h0t, wg2, wu2, wd2, wg, wu, wd, mg, mu, md, vg, vu, vd,
-     og, ou, od, omg, omu, omd, ovg, ovu, ovd, kept,
+    (x_in, dy_in, wg2, wu2, wd2, wg, wu, wd, mg, mu, md, vg, vu, vd,
+     og, ou, od, omg, omu, omd, ovg, ovu, ovd, kept, a0, a0t, h0t,
      L, R1, R1c, R2, MV, W, NW, D, R1d, R2d, MVd, Wd, NWd, A, AT, DY, DA, HT, DGU, TW, TD,
-     ss, rs, ssd, rsd, ls, lsd, lt, la, lk, lh) = refs
+     ss, rs, ssd, rsd, ls, lsd, lt, la, lk, lh, lx) = refs
     tokens, d = A.shape
     block = 1024
     rep, me = lax.axis_index("rep"), lax.axis_index("dp")
@@ -35,14 +35,9 @@
     def at(dx, dy):
         return (rep, xs[dx % side] * side + ys[dy % side])
 
-    for src, dst, n in ((a1, A, 0), (dy_in, DY, 1), (a1t, AT, 2)):
-        pltpu.make_async_copy(src, dst, la.at[n]).start()
     barrier = pltpu.get_barrier_semaphore()
     for dx, dy in ((1, 0), (-1, 0), (0, 1), (0, -1)):
         pl.semaphore_signal(barrier, inc=1, device_id=at(dx, dy), device_id_type=MESH)
-    DA[...] = jnp.zeros_like(DA)
-    pl.semaphore_wait(barrier, 4)
-
     def tile_of(c, t):
         g = 2 * t + c // 2
         past = g >= tiles
@@ -77,10 +72,10 @@
         fl.local = lambda c, t: D.at[t, :, :, :, :, lane(c)]
         fl.r1 = lambda c, t, s: R1d.at[ab, c, s]
         fl.r2 = lambda c, t, s: R2d.at[ab, c, s]
-        fl.nw = lambda c, t: NWd.at[ab, c]
+        fl.nw = lambda c, t: NWd.at[c]
         fl.sems = lambda c, t, k: (ssd.at[ab, c, k], rsd.at[ab, c, k])
-        fl.mv = lambda c, t: (MVd.at[ab, c, 0], MVd.at[ab, c, 1])
-        fl.w = lambda c, t: Wd.at[ab, c]
+        fl.mv = lambda c, t: (MVd.at[c, 0], MVd.at[c, 1])
+        fl.w = lambda c, t: Wd.at[c]
         fl.ls = lambda c, t, k: lsd.at[ab, c, k]
         fl.out = lambda c, t: od.at[t, :, :, :, :, lane(c)]
 
@@ -179,8 +174,106 @@
         return loads + ([pltpu.make_async_copy(wd2.at[layer, cols, :], TD.at[par], lt.at[par, 2])] if down else [])
 
     def state_load(n):
-        src, dst = ((a1, A), (dy_in, DY), (a1t, AT), (h1, A), (a0, A), (a0t, AT))[n]
+        src, dst = ((dy_in, DY), (a0, A), (a0t, AT))[n]
         return pltpu.make_async_copy(src, dst, la.at[n])
+
+    each = tokens // (side * side * 16)
+
+    def forth():
+        part = tokens // side
+
+        def down_load(j):
+            cols = pl.ds(pl.multiple_of(j * TILE, TILE), TILE)
+            return [pltpu.make_async_copy(wd2.at[0, cols, :], TD.at[lax.rem(j, 3)], lt.at[lax.rem(j, 2), 2])]
+
+        def loads(j):
+            return tile_loads(0, j, lax.rem(j, 2), False) + down_load(j)
+
+        def x_load(n):
+            return pltpu.make_async_copy(x_in.at[n], D.at[0, n, :, pl.ds(0, each)], lx.at[n])
+
+        def hidden_out(j):
+            rows = pl.ds(pl.multiple_of(j * TILE, TILE), TILE)
+            return pltpu.make_async_copy(HT.at[lax.rem(j, 2)], h0t.at[rows, :], lh.at[lax.rem(j, 2)])
+
+        def norm(rows, h):
+            a = (h * lax.rsqrt(jnp.mean(h * h, -1, keepdims=True) + 1e-6)).astype(BF)
+            A[rows, :] = a
+            AT[:, rows] = a.T
+
+        for n in range(side):
+            x_load(n).start()
+        for one in loads(0):
+            one.start()
+        state_load(0).start()
+        DA[...] = jnp.zeros_like(DA)
+        DGU[1, :, :TILE] = jnp.zeros((tokens, TILE), BF)
+        TD[2] = jnp.zeros((TILE, d), BF)
+
+        def begin(n, carry):
+            x_load(n).wait()
+            norm(pl.ds(pl.multiple_of(n * part, part), part), D[0, n, :, :each].reshape(part, d).astype(F32))
+            return carry
+
+        lax.fori_loop(0, side, begin, 0)
+        outs = [pltpu.make_async_copy(A, a0, la.at[1]), pltpu.make_async_copy(AT, a0t, la.at[2])]
+        for one in outs:
+            one.start()
+
+        def turn(j, carry):
+            par = lax.rem(j, 2)
+
+            @pl.when(j + 1 < tiles)
+            def _():
+                for one in loads(j + 1):
+                    one.start()
+
+            for one in loads(j):
+                one.wait()
+
+            @pl.when(j >= 2)
+            def _():
+                hidden_out(j - 2).wait()
+
+            def some(b, carry):
+                rows = pl.ds(pl.multiple_of(b * block, block), block)
+                both = dot(A[rows, :], TW[par], ((1,), (0,)))
+                DA[rows, :] += dot(DGU[1 - par, rows, :TILE], TD[lax.rem(j + 2, 3)], ((1,), (0,)))
+                gate, up = both[:, :TILE], both[:, TILE:]
+                hid = (gate * jax.nn.sigmoid(gate) * up).astype(BF)
+                DGU[par, rows, :TILE] = hid
+                HT[par, :, rows] = hid.T
+                return carry
+
+            lax.fori_loop(0, tokens // block, some, 0)
+            hidden_out(j).start()
+            return carry
+
+        lax.fori_loop(0, tiles, turn, 0)
+        for one in tile_loads(1, 0, 0):
+            one.start()
+
+        def last_down(b, carry):
+            rows = pl.ds(pl.multiple_of(b * block, block), block)
+            DA[rows, :] += dot(DGU[(tiles - 1) % 2, rows, :TILE], TD[(tiles - 1) % 3], ((1,), (0,)))
+            return carry
+
+        lax.fori_loop(0, tokens // block, last_down, 0)
+        for one in outs:
+            one.wait()
+        hidden_out(tiles - 2).wait()
+        hidden_out(tiles - 1).wait()
+
+        def end(n, carry):
+            rows = pl.ds(pl.multiple_of(n * part, part), part)
+            h = (D[0, n, :, :each].reshape(part, d).astype(F32) + DA[rows, :].astype(BF).astype(F32)).astype(BF)
+            D[0, n, :, :each] = h.reshape(side, each, 16, d)
+            DA[rows, :] = jnp.zeros((part, d), F32)
+            norm(rows, h.astype(F32))
+            return carry
+
+        lax.fori_loop(0, side, end, 0)
+        state_load(0).wait()
 
     def keep(j, par):
         return pltpu.make_async_copy(DGU.at[par], kept.at[j], lk.at[par])
@@ -230,9 +323,10 @@
         lax.fori_loop(0, tokens // block, some, 0)
 
     def norm_back():
-        def some(b, carry):
-            rows = pl.ds(pl.multiple_of(b * 256, 256), 256)
-            h = A[rows, :].astype(F32)
+        def some(n, carry):
+            size = each * 16
+            rows = pl.ds(pl.multiple_of(n * size, size), size)
+            h = D[0, lax.div(n, side), lax.rem(n, side), :each].reshape(size, d).astype(F32)
             scale = lax.rsqrt(jnp.mean(h * h, -1, keepdims=True) + 1e-6)
             da = DA[rows, :].astype(BF).astype(F32)
             inner = jnp.mean(h * da, -1, keepdims=True)
@@ -240,7 +334,7 @@
             DY[rows, :] = (DY[rows, :].astype(F32) + back.astype(F32)).astype(BF)
             return carry
 
-        lax.fori_loop(0, tokens // 256, some, 0)
+        lax.fori_loop(0, side * side, some, 0)
 
     def compute(q):
         turn, part = lax.div(q, 3), lax.rem(q, 3)
@@ -303,8 +397,8 @@
             @pl.when(p == 0)
             def _():
                 keep(tiles - 2, 1).wait()
-                state_load(3).start()
-                state_load(5).start()
+                state_load(1).start()
+                state_load(2).start()
 
             @pl.when(p > 0)
             def _():
@@ -325,14 +419,12 @@
             hidden_load(0).start()
             for one in tile_loads(0, 0, tiles % 2):
                 one.start()
-            state_load(3).wait()
             norm_back()
-            state_load(4).start()
 
         @pl.when(q == 3 * (tiles + middle) - 1)
         def _():
-            state_load(4).wait()
-            state_load(5).wait()
+            state_load(1).wait()
+            state_load(2).wait()
 
     def subround(q):
         six = lax.div(q, 6)
@@ -352,157 +444,35 @@
                             for c in (2 * (z % 2), 2 * (z % 2) + 1):
                                 stage(gu, c, lax.div(g, 2), k)
 
-        for ab in (0, 1):
-
-            @pl.when((q >= 3 * tiles) & (lax.rem(q, 2) == (tiles + ab) % 2))
+        for ab, at1, at0 in ((0, 3 * tiles + 4, 3 * (tiles + middle) + 10), (1, 3 * tiles + 11, 3 * (tiles + middle) + 29)):
+
+            @pl.when((q >= at1) & (lax.rem(q, 2) == at1 % 2))
             def _():
                 for k in range(12, -1, -1):
-                    at1, at0 = 3 * tiles + ab + 2 * k, 3 * (tiles + middle) + ab + 2 * k
-
-                    @pl.when((q == at1) | (q == at0))
+                    now1, now0 = q == at1 + 2 * k, q == at0 + 2 * k
+
+                    @pl.when(now1 | now0)
                     def _():
                         for c in range(4):
-                            stage(downs[ab], c, jnp.where(q == at1, 1, 0), k)
+                            stage(downs[ab], c, jnp.where(now1, 1, 0), k)
 
     def body(q, carry):
         compute(q)
         subround(q)
         return carry
 
-    for one in tile_loads(1, 0, 0):
-        one.start()
-    for n in range(3):
-        state_load(n).wait()
+    forth()
+    pl.semaphore_wait(barrier, 4)
     lax.fori_loop(0, 3 * last + 2 + 2 * 12, body, 0)
-
-
-def first_kernel(tiles, x_in, wg2, wu2, wd2, h1, a1, a1t, a0, a0t, h0t, X, A, AT, ACC, HN, HT, TW, TD, lt, lx, lh, lo):
-    tokens, d = X.shape
-    block, part = 1024, 512
-
-    def tile_loads(j):
-        par = lax.rem(j, 2)
-        cols = pl.ds(pl.multiple_of(j * TILE, TILE), TILE)
-        return (pltpu.make_async_copy(wg2.at[0, :, cols], TW.at[par, :, :TILE], lt.at[par, 0]),
-                pltpu.make_async_copy(wu2.at[0, :, cols], TW.at[par, :, TILE:], lt.at[par, 1]),
-                pltpu.make_async_copy(wd2.at[0, cols, :], TD.at[lax.rem(j, 3)], lt.at[par, 2]))
-
-    def x_load(n):
-        rows = pl.ds(pl.multiple_of(n * part, part), part)
-        return pltpu.make_async_copy(x_in.at[rows, :], X.at[rows, :], lx.at[n])
-
-    def hidden_out(j):
-        return pltpu.make_async_copy(HT.at[j % 2], h0t.at[pl.ds(pl.multiple_of(j * TILE, TILE), TILE), :], lh.at[j % 2])
-
-    def norm(rows, h):
-        a = (h * lax.rsqrt(jnp.mean(h * h, -1, keepdims=True) + 1e-6)).astype(BF)
-        A[rows, :] = a
-        AT[:, rows] = a.T
-
-    for n in range(tokens // part):
-        x_load(n).start()
-    for one in tile_loads(0):
-        one.start()
-    ACC[...] = jnp.zeros_like(ACC)
-    HN[1] = jnp.zeros((tokens, TILE), BF)
-    TD[2] = jnp.zeros((TILE, d), BF)
-
-    def begin(n, carry):
-        x_load(n).wait()
-        rows = pl.ds(pl.multiple_of(n * part, part), part)
-        norm(rows, X[rows, :].astype(F32))
-        return carry
-
-    lax.fori_loop(0, tokens // part, begin, 0)
-    outs = [pltpu.make_async_copy(A, a0, lo.at[0]), pltpu.make_async_copy(AT, a0t, lo.at[1])]
-    for one in outs:
-        one.start()
-
-    def turn(j, carry):
-        par = j % 2
-
-        @pl.when(j + 1 < tiles)
-        def _():
-            for one in tile_loads(j + 1):
-                one.start()
-
-        for one in tile_loads(j):
-            one.wait()
-
-        @pl.when(j >= 2)
-        def _():
-            hidden_out(j - 2).wait()
-
-        def some(b, carry):
-            rows = pl.ds(pl.multiple_of(b * block, block), block)
-            both = dot(A[rows, :], TW[par], ((1,), (0,)))
-            ACC[rows, :] += dot(HN[1 - par, rows, :], TD[lax.rem(j + 2, 3)], ((1,), (0,)))
-            gate, up = both[:, :TILE], both[:, TILE:]
-            hid = (gate * jax.nn.sigmoid(gate) * up).astype(BF)
-            HN[par, rows, :] = hid
-            HT[par, :, rows] = hid.T
-            return carry
-
-        lax.fori_loop(0, tokens // block, some, 0)
-        hidden_out(j).start()
-        return carry
-
-    lax.fori_loop(0, tiles, turn, 0)
-
-    def last_down(b, carry):
-        rows = pl.ds(pl.multiple_of(b * block, block), block)
-        ACC[rows, :] += dot(HN[(tiles - 1) % 2, rows, :], TD[(tiles - 1) % 3], ((1,), (0,)))
-        return carry
-
-    lax.fori_loop(0, tokens // block, last_down, 0)
-    for one in outs:
-        one.wait()
-    hidden_out(tiles - 2).wait()
-    hidden_out(tiles - 1).wait()
-
-    def end(n, carry):
-        rows = pl.ds(pl.multiple_of(n * part, part), part)
-        h = (X[rows, :].astype(F32) + ACC[rows, :].astype(BF).astype(F32)).astype(BF)
-        X[rows, :] = h
-        norm(rows, h.astype(F32))
-        return carry
-
-    lax.fori_loop(0, tokens // part, end, 0)
-    outs = [pltpu.make_async_copy(A, a1, lo.at[0]), pltpu.make_async_copy(AT, a1t, lo.at[1]), pltpu.make_async_copy(X, h1, lo.at[2])]
-    for one in outs:
-        one.start()
-    for one in outs:
-        one.wait()
-
-
-def first(x, wg, wu, wd):
-    tokens, d = x.shape
-    ff = wg.shape[2]
-    tiles = ff // TILE
-    hbm = pl.BlockSpec(memory_space=pl.ANY)
-    dma = pltpu.SemaphoreType.DMA
-    wide, tall, hid = (jax.ShapeDtypeStruct(t, BF) for t in ((tokens, d), (d, tokens), (ff, tokens)))
-    return pl.pallas_call(
-        functools.partial(first_kernel, tiles),
-        out_shape=[wide, wide, tall, wide, tall, hid],
-        in_specs=[hbm] * 4,
-        out_specs=[hbm] * 6,
-        scratch_shapes=[
-            pltpu.VMEM((tokens, d), BF), pltpu.VMEM((tokens, d), BF), pltpu.VMEM((d, tokens), BF), pltpu.VMEM((tokens, d), F32),
-            pltpu.VMEM((2, tokens, TILE), BF), pltpu.VMEM((2, TILE, tokens), BF),
-            pltpu.VMEM((2, d, 2 * TILE), BF), pltpu.VMEM((3, TILE, d), BF),
-            dma((2, 3)), dma((4,)), dma((2,)), dma((3,)),
-        ],
-        compiler_params=pltpu.CompilerParams(vmem_limit_bytes=60 * 2**20),
-        name="first",
-    )(x, wg, wu, wd)
 
 
 def synced(mesh, states, ws, ms, vs):
     n = mesh.shape["dp"]
     side = math.isqrt(n)
     layers, d, ff = ws[0].shape
-    tokens = states[0].shape[0]
+    x, dy = states
+    tokens = x.shape[0]
+    x = x.reshape(side, side, -1, 16, d)
     tiles = ff // TILE
     rows, per = d // n, ff // n // 16
     gu, dn = (rows, TILE), (per, 16, 128)
@@ -511,7 +481,7 @@
     ws5 = [w.reshape(layers, side, side, *mat) for w, mat in zip(ws, mats)]
     mvs = [t.reshape(layers, *mat) for t, mat in zip((*ms, *vs), mats * 2)]
     out_shape = [jax.ShapeDtypeStruct(w.shape, BF) for w in ws5] + [jax.ShapeDtypeStruct(t.shape, F32) for t in mvs]
-    out_shape.append(jax.ShapeDtypeStruct((tiles, tokens, 2 * TILE), BF))
+    out_shape += [jax.ShapeDtypeStruct(t, BF) for t in ((tiles, tokens, 2 * TILE), (tokens, d), (d, tokens), (ff, tokens))]
     dma = pltpu.SemaphoreType.DMA
     scratch = [
         pltpu.VMEM((3, 4, side, side, *gu), BF),
@@ -524,9 +494,9 @@
         pltpu.VMEM((layers, side, side, per, 16, d), BF),
         pltpu.VMEM((2, 4, 3, side, *dn), BF),
         pltpu.VMEM((2, 4, 3, *dn), BF),
-        pltpu.VMEM((2, 4, 2, *dn), F32),
-        pltpu.VMEM((2, 4, *dn), BF),
-        pltpu.VMEM((2, 4, *dn), BF),
+        pltpu.VMEM((4, 2, *dn), F32),
+        pltpu.VMEM((4, *dn), BF),
+        pltpu.VMEM((4, *dn), BF),
         pltpu.VMEM((tokens, d), BF),
         pltpu.VMEM((d, tokens), BF),
         pltpu.VMEM((tokens, d), BF),
@@ -534,27 +504,26 @@
         pltpu.VMEM((2, TILE, tokens), BF),
         pltpu.VMEM((2, tokens, 2 * TILE), BF),
         pltpu.VMEM((2, d, 2 * TILE), BF),
-        pltpu.VMEM((2, TILE, d), BF),
+        pltpu.VMEM((3, TILE, d), BF),
         dma((2, 4, 12)), dma((2, 4, 12)), dma((2, 4, 12)), dma((2, 4, 12)),
-        dma((4, 6)), dma((2, 4, 6)), dma((2, 3)), dma((6,)), dma((2,)), dma((2,)),
+        dma((4, 6)), dma((2, 4, 6)), dma((2, 3)), dma((3,)), dma((2,)), dma((2,)), dma((side,)),
     ]
     res = pl.pallas_call(
         functools.partial(sync_kernel, side, tiles),
         out_shape=out_shape,
-        in_specs=[hbm] * 19,
-        out_specs=[hbm] * 10,
+        in_specs=[hbm] * 14,
+        out_specs=[hbm] * 13,
         scratch_shapes=scratch,
         compiler_params=pltpu.CompilerParams(collective_id=0, has_side_effects=True, vmem_limit_bytes=67043328),
         name="sync",
-    )(*states, *ws, *ws5, *mvs)
+    )(x, dy, *ws, *ws5, *mvs)
     return [r.reshape(w.shape) for r, w in zip(res[:9], (*ws, *ms, *vs))]
 
 
 def solution(mesh):
     def step(x, dy, wg, wu, wd, *mv):
         x, dy = x[0], dy[0]
-        h1, a1, a1t, a0, a0t, h0t = first(x, wg, wu, wd)
-        states = (a1, a1t, a0, a0t, dy, h1, h0t)
+        states = (x, dy)
         return tuple(synced(mesh, states, (wg, wu, wd), mv[:3], mv[3:]))
 
     rd, rep, shard = P(("rep", "dp")), P(), P(None, "dp", None)

time: 515 us -> 500 us (0.971)
  Pallas kernels: 483 us -> 465 us
    pallas_call x1 -> x0, Pallas kernels: 53.7 us -> none  [first(): pl.pallas_call(functools.partial(first_kernel, tiles), out_shape=[wide, w...]
    pallas_call x1, Pallas kernels: 430 us -> 465 us  [synced(): pl.pallas_call(functools.partial(sync_kernel, side, tiles), out_shape=out...]
where the time goes in v4:
time: 500 us
  Pallas kernels  465 us (93%)
  local copies, waits for them, and re-layouts  34.5 us (7%)
    pallas_call x1, Pallas kernels, synced(): pl.pallas_call(functools.partial(sync_kernel, side, tiles), out_shape=out...  465 us
    unnamed x29, local copies, waits for them, and re-layouts  34.5 us

profile of v4, /device:TPU:96, one launch (start us, length us, event | category | flops | bytes accessed | tf_op | source)
XLA Modules:
  0.0 500.0 jit_solution(7673940226246235248)
XLA Ops:
  0.6 464.8 %sync.1 = (bf16[2,4,4,64,2816]{4,3,2,1,0:T(8,128)(2,1)}, bf16[2,4,4,64,2816]{4,3,2,1,0:T(8,128)(2,1)}, bf16[2,4,4,11,16,1024]{5,4,3,2,1,0:T(8,128)(2,1)}, f32[2,...) custom-call(bf16[4,4,8,16,1024]{4,3,2,1,0:T(8,128)(2,1)} %bitcast.20, ...), custom_call_target="tpu_custom_call" | custom-call | tf_op jit(solution)/shard_map/sync/pallas_call | solution.py:511
  465.4 0.0 copy-start
  465.5 0.0 slice-start
  465.5 0.0 slice-start.1
  465.5 11.7 %copy.29 = bf16[2,1024,2816]{2,1,0:T(8,128)(2,1)} copy(bf16[2,1024,2816]{2,1,0:T(8,128)(2,1)} %bitcast.19) | data formatting | bytes 23068672
  477.2 0.0 copy-done
  477.2 0.0 slice-start.2
  477.2 5.8 %copy.30 = bf16[2,1024,2816]{2,1,0:T(8,128)(2,1)} copy(bf16[2,1024,2816]{2,1,0:T(8,128)(2,1)S(1)} %bitcast.18) | data formatting | bytes 23068672
  483.0 0.0 slice-done
  483.0 0.7 slice-done.1
  483.7 1.3 slice-done.2
  485.0 0.0 copy-start.6
  485.0 4.4 copy.31
  489.4 0.0 copy-done.6
  489.4 0.0 copy-start.5
  489.4 1.1 copy.32
  490.5 0.8 copy-done.5
  491.3 0.0 copy-start.4
  491.3 1.1 copy.33
  492.4 0.8 copy-done.4
  493.2 0.0 copy-start.3
  493.2 1.1 copy.34
  494.3 0.8 copy-done.3
  495.1 0.0 copy-start.2
  495.1 1.1 copy.35
  496.2 0.8 copy-done.2
  497.0 0.0 copy-start.1
  497.0 1.1 copy.36
  498.1 0.8 copy-done.1
  498.9 1.1 copy.37
  (1 shorter events, 0.0 us)
Async XLA Ops:
  465.4 11.7 %copy-start = (bf16[2,4,4,64,2816]{4,3,2,1,0:T(8,128)(2,1)S(1)}, bf16[2,4,4,64,2816]{4,3,2,1,0:T(8,128)(2,1)}, u32[]{:S(2)}) copy-start(bf16[2,4,4,64,2816]{4,3,2,1,0:T(8,128)(2,1)} %get-tuple-element.19) | copy-start | bytes 34603012
  465.5 17.6 %slice-start = ((s8[11534336]{0:T(1024)(128)(4,1)}), s8[4194304]{0:T(1024)(128)(4,1)S(1)}, s32[]{:S(2)}) async-start(s8[11534336]{0:T(1024)(128)(4,1)} %bitcast.15), calls=%async_computation | async-start | bytes 8388608
  465.5 18.2 %slice-start.1 = ((s8[11534336]{0:T(1024)(128)(4,1)}), s8[4194304]{0:T(1024)(128)(4,1)S(1)}, s32[]{:S(2)}) async-start(s8[11534336]{0:T(1024)(128)(4,1)} %bitcast.15), calls=%async_computation.1 | async-start | bytes 8388608
  477.2 7.8 %slice-start.2 = ((s8[11534336]{0:T(1024)(128)(4,1)}), s8[3145728]{0:T(1024)(128)(4,1)S(1)}, s32[]{:S(2)}) async-start(s8[11534336]{0:T(1024)(128)(4,1)} %bitcast.15), calls=%async_computation.2 | async-start | bytes 6291456
  485.0 4.4 copy-start.6
  489.4 1.9 copy-start.5
  491.3 1.9 copy-start.4
  493.2 1.9 copy-start.3
  495.1 1.9 copy-start.2
  497.0 1.9 copy-start.1
